TPU v7x, 16 devices: a whole 2x2x2 slice. The times are simulated.
16 devices in a mesh: data: 16 (over z, y, x, core).
Axes of the slice: x: 2, y: 2, z: 2, core: 2. Of those that a mesh axis runs over, the one named last changes fastest.
Arguments:
- tokens: bfloat16 [16384, 1536], P('data')
- targets: bfloat16 [16384, 1536], P('data')
- w_in: bfloat16 [2, 1536, 8960], replicated
- w_out: bfloat16 [2, 8960, 1536], replicated
Outputs:
- output 1: float32 [2, 1536, 8960], P(None, 'data')
- output 2: float32 [2, 8960, 1536], P(None, 'data')
All inputs are finite; a program needn't handle non-finite values.
Results may differ from a plain program's by a relative error of at most 0.00605358.
Values are sent between devices in bfloat16 or wider.
A program may use at most 1 GiB of HBM per device.

v0:
```python
import jax
import jax.numpy as jnp
from jax import lax
from jax.sharding import PartitionSpec as P


def gelu_act(pre_f32):
    return jax.nn.gelu(pre_f32, approximate=True)


def solution(mesh):
    data_size = mesh.shape["data"]

    def local_grads(tokens, targets, w_in, w_out):
        layers = w_in.shape[0]
        scale = (tokens.shape[0] * data_size) ** -0.5
        hidden = tokens
        saved_fwd = []
        for layer in range(layers):
            pre_act = jnp.dot(hidden, w_in[layer], preferred_element_type=jnp.float32).astype(jnp.bfloat16)
            act_out = gelu_act(pre_act.astype(jnp.float32)).astype(jnp.bfloat16)
            branch = jnp.dot(act_out, w_out[layer], preferred_element_type=jnp.float32)
            saved_fwd.append((hidden, pre_act, act_out))
            hidden = (hidden.astype(jnp.float32) + branch).astype(jnp.bfloat16)
        grad_h = ((hidden.astype(jnp.float32) - targets.astype(jnp.float32)) * scale).astype(jnp.bfloat16)
        shares_first = [None] * layers
        shares_second = [None] * layers
        for layer in reversed(range(layers)):
            hidden_in, pre_act, act_out = saved_fwd[layer]
            grad_second = jnp.einsum("tf,td->fd", act_out, grad_h, preferred_element_type=jnp.float32)
            shares_second[layer] = lax.psum_scatter(grad_second, "data", scatter_dimension=0, tiled=True)
            grad_act = jnp.einsum("td,fd->tf", grad_h, w_out[layer], preferred_element_type=jnp.float32).astype(jnp.bfloat16)
            _, pullback = jax.vjp(gelu_act, pre_act.astype(jnp.float32))
            grad_pre = pullback(grad_act.astype(jnp.float32))[0].astype(jnp.bfloat16)
            grad_first = jnp.einsum("td,tf->df", hidden_in, grad_pre, preferred_element_type=jnp.float32)
            shares_first[layer] = lax.psum_scatter(grad_first, "data", scatter_dimension=0, tiled=True)
            if layer > 0:
                grad_below = jnp.einsum("tf,df->td", grad_pre, w_in[layer], preferred_element_type=jnp.float32)
                grad_h = (grad_h.astype(jnp.float32) + grad_below).astype(jnp.bfloat16)
        return jnp.stack(shares_first), jnp.stack(shares_second)

    tok_spec = P("data", None)
    grad_spec = P(None, "data", None)
    return jax.shard_map(local_grads, mesh=mesh, in_specs=(tok_spec, tok_spec, P(), P()), out_specs=(grad_spec, grad_spec), check_vma=False)
```

profile of v0, /device:TPU:0, one launch (start us, length us, event | category | flops | bytes accessed | tf_op | source)
XLA Modules:
  0.0 1347.0 jit_solution(4074821046897008488)
XLA Ops:
  7.2 37.9 %fusion.55 = bf16[1024,8960]{1,0:T(8,128)(2,1)} fusion(bf16[1024,1536]{1,0:T(8,128)(2,1)} %param.4, bf16[2,1536,8960]{2,1,0:T(8,128)(2,1)} %param.6), kind=kOutput, calls=%fused_computation.63 | convolution fusion | flops 28194897920 | bytes 49020928 | tf_op jit(solution)/shard_map/dot_general | solution.py:20
  45.1 36.8 %add_convert_fusion.2 = bf16[1024,1536]{1,0:T(8,128)(2,1)S(1)} fusion(bf16[1024,1536]{1,0:T(8,128)(2,1)S(1)} %copy-done.1, bf16[2,8960,1536]{2,1,0:T(8,128)(2,1)} %param.7, bf16[1024,8960]{1,0:T(8,128)(2,1)} %fusion.55), kind=kOutput, calls=%fused_computation.70 | convolution fusion | flops 28282191872 | bytes 52166656 | tf_op jit(solution)/shard_map/dot_general | solution.py:22
  81.9 35.7 %fusion.58 = bf16[1024,8960]{1,0:T(8,128)(2,1)} fusion(bf16[1024,1536]{1,0:T(8,128)(2,1)S(1)} %add_convert_fusion.2, bf16[2,1536,8960]{2,1,0:T(8,128)(2,1)} %param.6), kind=kOutput, calls=%fused_computation.64 | convolution fusion | flops 28194897920 | bytes 49020928 | tf_op jit(solution)/shard_map/dot_general | solution.py:20
  117.6 37.6 %multiply_convert_fusion = bf16[1024,1536]{1,0:T(8,128)(2,1)S(1)} fusion(bf16[1024,1536]{1,0:T(8,128)(2,1)S(1)} %copy-done, bf16[2,8960,1536]{2,1,0:T(8,128)(2,1)} %param.7, bf16[1024,1536]{1,0:T(8,128)(2,1)S(1)} %add_convert_fusion.2, bf16[1024,8960]{1,0:T(8,128)(2,1)} %fusion.58), kind=kOutput, calls=%fused_computation.68 | convolution fusion | flops 28290056192 | bytes 55312384 | tf_op jit(solution)/shard_map/dot_general | solution.py:22
  155.2 53.7 %fusion.4 = bf16[1024,8960]{1,0:T(8,128)(2,1)} fusion(bf16[1024,8960]{1,0:T(8,128)(2,1)} %fusion.58, bf16[1024,1536]{1,0:T(8,128)(2,1)S(1)} %multiply_convert_fusion, bf16[2,8960,1536]{2,1,0:T(8,128)(2,1)} %param.7), kind=kOutput, calls=%fused_computation.17 | convolution fusion | flops 28396748800 | bytes 67371008 | tf_op jit(solution)/shard_map/td,fd->tf/dot_general | solution.py:32
  208.9 35.8 %fusion.83 = f32[1536,8960]{1,0:T(8,128)} fusion(bf16[1024,1536]{1,0:T(8,128)(2,1)S(1)} %add_convert_fusion.2, bf16[1024,8960]{1,0:T(8,128)(2,1)} %fusion.4), kind=kOutput, calls=%fused_computation.79 | convolution fusion | flops 28185722880 | bytes 76546048
  244.7 0.0 reduce-scatter.13.cloned.1.call-start
  244.8 35.9 %add_convert_fusion = bf16[1024,1536]{1,0:T(8,128)(2,1)} fusion(bf16[1024,1536]{1,0:T(8,128)(2,1)S(1)} %multiply_convert_fusion, bf16[1024,8960]{1,0:T(8,128)(2,1)} %fusion.4, bf16[2,1536,8960]{2,1,0:T(8,128)(2,1)} %param.6), kind=kOutput, calls=%fused_computation.67 | convolution fusion | flops 28190441472 | bytes 52166656 | tf_op jit(solution)/shard_map/tf,df->td/dot_general | solution.py:38
  280.7 56.2 %fusion.103 = bf16[1024,8960]{1,0:T(8,128)(2,1)} fusion(bf16[1024,8960]{1,0:T(8,128)(2,1)} %fusion.55, bf16[1024,1536]{1,0:T(8,128)(2,1)} %add_convert_fusion, bf16[2,8960,1536]{2,1,0:T(8,128)(2,1)} %param.7), kind=kOutput, calls=%fused_computation.20.clone.clone.1 | convolution fusion | flops 28396748800 | bytes 67371008 | tf_op jit(solution)/shard_map/td,fd->tf/dot_general | solution.py:32
  336.8 36.4 %convolution_bitcast_fusion = f32[1536,8960]{0,1:T(8,128)} fusion(bf16[1024,1536]{1,0:T(8,128)(2,1)S(1)} %copy-done.2, bf16[1024,8960]{1,0:T(8,128)(2,1)} %fusion.103), kind=kOutput, calls=%fused_computation.14 | convolution fusion | flops 28185722880 | bytes 76546048 | tf_op jit(solution)/shard_map/td,tf->df/dot_general | solution.py:35
  373.2 55.6 %copy.11 = f32[1536,8960]{1,0:T(8,128)} copy(f32[1536,8960]{0,1:T(8,128)} %convolution_bitcast_fusion) | data formatting | bytes 110100480
  428.9 0.0 reduce-scatter.9.cloned.1.call-start
  428.9 2.4 copy-done.5
  431.3 43.1 %fusion.80 = f32[8960,1536]{1,0:T(8,128)} fusion(bf16[1024,1536]{1,0:T(8,128)(2,1)S(1)} %copy-done.5, bf16[1024,8960]{1,0:T(8,128)(2,1)} %fusion.55), kind=kOutput, calls=%fused_computation.78 | convolution fusion | flops 28277473280 | bytes 76546048 | tf_op jit(solution)/shard_map/tf,td->fd/dot_general | solution.py:30
  474.5 1.8 copy-done.4
  476.3 43.3 %fusion.77 = f32[8960,1536]{1,0:T(8,128)} fusion(bf16[1024,1536]{1,0:T(8,128)(2,1)S(1)} %copy-done.4, bf16[1024,8960]{1,0:T(8,128)(2,1)} %fusion.58), kind=kOutput, calls=%fused_computation.77 | convolution fusion | flops 28277473280 | bytes 76546048 | tf_op jit(solution)/shard_map/tf,td->fd/dot_general | solution.py:30
  519.7 5.4 copy.14
  525.0 263.0 %reduce-scatter.13.cloned.1.call-done = f32[96,8960]{1,0:T(8,128)} async-done(((f32[1536,8960]{1,0:T(8,128)}), f32[96,8960]{1,0:T(8,128)}) %reduce-scatter.13.cloned.1.call-update) | async-done | bytes 3440656
  788.0 5.3 copy.12
  793.4 6.8 pad_maximum_fusion
  800.2 9.9 copy.9
  810.1 250.8 %reduce-scatter.9.cloned.1.call-done = f32[560,1536]{1,0:T(8,128)} async-done(((f32[8960,1536]{1,0:T(8,128)}), f32[560,1536]{1,0:T(8,128)}) %reduce-scatter.9.cloned.1.call-update) | async-done | bytes 3440656 | tf_op jit(solution)/shard_map/reduce_scatter | solution.py:31
  1060.9 272.7 %reduce-scatter.11.cloned.1.call-done = f32[560,1536]{1,0:T(8,128)} async-done(((f32[8960,1536]{1,0:T(8,128)}), f32[560,1536]{1,0:T(8,128)}) %reduce-scatter.11.cloned.1.call-update) | async-done | bytes 3440656 | tf_op jit(solution)/shard_map/reduce_scatter | solution.py:31
  1333.6 6.4 pad_maximum_fusion.1
  (17 shorter events, 0.2 us)
Async XLA Ops:
  7.2 37.9 %copy-start.1 = (bf16[1024,1536]{1,0:T(8,128)(2,1)S(1)}, bf16[1024,1536]{1,0:T(8,128)(2,1)}, u32[]{:S(2)}) copy-start(bf16[1024,1536]{1,0:T(8,128)(2,1)} %param.4) | copy-start | bytes 9437188
  7.2 512.5 %reduce-scatter.15.cloned.1.call-start = ((), (), s32[]{:S(2)}) async-start(), calls=%async_computation.7 | async-start | bytes 58490880
  81.9 35.7 %copy-start = (bf16[1024,1536]{1,0:T(8,128)(2,1)S(1)}, bf16[1024,1536]{1,0:T(8,128)(2,1)}, u32[]{:S(2)}) copy-start(bf16[1024,1536]{1,0:T(8,128)(2,1)} %param.5) | copy-start | bytes 9437188
  155.2 89.6 %copy-start.3 = (bf16[1024,1536]{1,0:T(8,128)(2,1)}, bf16[1024,1536]{1,0:T(8,128)(2,1)S(1)}, u32[]{:S(2)}) copy-start(bf16[1024,1536]{1,0:T(8,128)(2,1)S(1)} %multiply_convert_fusion) | copy-start | bytes 9437188
  244.7 543.3 %reduce-scatter.13.cloned.1.call-start = ((), (), s32[]{:S(2)}) async-start(), calls=%async_computation.6 | async-start | bytes 58490880
  280.7 56.2 %copy-start.2 = (bf16[1024,1536]{1,0:T(8,128)(2,1)S(1)}, bf16[1024,1536]{1,0:T(8,128)(2,1)}, u32[]{:S(2)}) copy-start(bf16[1024,1536]{1,0:T(8,128)(2,1)} %param.4) | copy-start | bytes 9437188
  428.8 2.5 copy-start.5
  428.9 632.0 %reduce-scatter.9.cloned.1.call-start = ((), (), s32[]{:S(2)}) async-start(), calls=%async_computation.4 | async-start | bytes 58490880 | tf_op jit(solution)/shard_map/reduce_scatter | solution.py:31
  474.4 1.9 copy-start.4
  474.4 859.1 %reduce-scatter.11.cloned.1.call-start = ((), (), s32[]{:S(2)}) async-start(), calls=%async_computation.5 | async-start | bytes 58490880 | tf_op jit(solution)/shard_map/reduce_scatter | solution.py:31
Sparse Core Ops, SparseCore 0:
  244.9 270.2 reduce-scatter.14
  520.5 267.5 reduce-scatter.12
  793.3 267.5 reduce-scatter.8
  1066.0 267.5 reduce-scatter.10
where the time goes:
time: 1350 us
  waiting for transfers between devices  787 us (58%)
  matrix products  452 us (33%)
  local copies, waits for them, and re-layouts  80.5 us (6%)
  between operations  14.3 us (1%)
    reduce_scatter x2, waiting for transfers between devices, local_grads(): lax.psum_scatter(grad_second, 'data', scatter_dimension=0, tiled=True)  523 us
    unnamed x6, waiting for transfers between devices  263 us
    dot_general x2, matrix products, local_grads(): jnp.einsum('td,fd->tf', grad_h, w_out[layer], preferred_element_type=jnp....  110 us
    dot_general x2, matrix products, local_grads(): jnp.einsum('tf,td->fd', act_out, grad_h, preferred_element_type=jnp.float32)  86.4 us
    unnamed x16, local copies, waits for them, and re-layouts  80.5 us
    dot_general x2, matrix products, local_grads(): branch = jnp.dot(act_out, w_out[layer], preferred_element_type=jnp.float32)  74.4 us
    dot_general x2, matrix products, local_grads(): jnp.dot(hidden, w_in[layer], preferred_element_type=jnp.float32)  73.5 us
    dot_general x1, matrix products, local_grads(): jnp.einsum('td,tf->df', hidden_in, grad_pre, preferred_element_type=jnp.f...  36.4 us
  transfers between devices with their start and end apart: 4, of which 3 were waited for; matrix products, arithmetic and copies ran while one was open for 22% of the time, Pallas kernels for 0%

commit v1 on v0

v1 whole, which is shorter than its diff:
```python
import functools

import jax
import jax.numpy as jnp
from jax import lax
from jax.experimental import pallas as pl
from jax.experimental.pallas import tpu as pltpu
from jax.sharding import PartitionSpec as P


AXIS = "data"
DEVICES = 16
CORE, X, Y, Z = 1, 2, 4, 8
GELU_S = 0.7978845608028654
GELU_C = 0.044715


def groups_of(bits):
    spans = []
    for base in range(DEVICES):
        if base & bits == 0:
            spans.append([base | sub for sub in range(DEVICES) if sub & ~bits == 0])
    return spans


def swap(value, bits):
    return lax.ppermute(value, AXIS, [(i, i ^ bits) for i in range(DEVICES)])


def gelu_parts(u):
    sq = u * u
    th = jnp.tanh(u * (GELU_S + (GELU_S * GELU_C) * sq))
    cdf = 0.5 + 0.5 * th
    slope = cdf + (0.5 * u) * (1.0 - th * th) * (GELU_S + (3.0 * GELU_S * GELU_C) * sq)
    return u * cdf, slope


def rounded(value):
    return value.astype(jnp.bfloat16).astype(jnp.float32)


def dot_nn(a, b):
    return jnp.dot(a, b, preferred_element_type=jnp.float32)


def dot_nt(a, b):
    return lax.dot_general(a, b, (((1,), (1,)), ((), ())), preferred_element_type=jnp.float32)


def forward_body(scale, parts, *refs):
    if scale is None:
        hidden, w_in, w_out, out, acc = refs
    else:
        hidden, w_in, w_out, target, pre_out, out, acc = refs
    step = pl.program_id(0)
    rows = hidden.shape[0] // parts

    @pl.when(step == 0)
    def _():
        acc[...] = hidden[...].astype(jnp.float32)

    for part in range(parts):
        at = pl.ds(part * rows, rows)
        pre = dot_nn(hidden[at], w_in[0]).astype(jnp.bfloat16)
        if scale is not None:
            pre_out[at] = pre
        act = gelu_parts(pre.astype(jnp.float32))[0].astype(jnp.bfloat16)
        acc[at] += dot_nn(act, w_out[0])

    @pl.when(step == pl.num_programs(0) - 1)
    def _():
        if scale is None:
            out[...] = acc[...].astype(jnp.bfloat16)
        else:
            out[...] = ((rounded(acc[...]) - target[...].astype(jnp.float32)) * scale).astype(jnp.bfloat16)


FF_TILE = 1280


def layer_specs(layer, rows, width):
    whole = pl.BlockSpec((rows, width), lambda j: (0, 0))
    w_in = pl.BlockSpec((1, width, FF_TILE), lambda j: (layer, 0, j))
    w_out = pl.BlockSpec((1, FF_TILE, width), lambda j: (layer, j, 0))
    pre = pl.BlockSpec((rows, FF_TILE), lambda j: (0, j))
    return whole, w_in, w_out, pre


def layer_params(rows, width, ff):
    return dict(
        compiler_params=pltpu.CompilerParams(vmem_limit_bytes=62 * 2**20, dimension_semantics=("arbitrary",)),
        cost_estimate=pl.CostEstimate(flops=4 * rows * width * ff, bytes_accessed=4 * width * ff, transcendentals=rows * ff),
    )


def layer_forward(hidden, w_in, w_out, layer, target=None, scale=None):
    (rows, width), ff = hidden.shape, w_in.shape[2]
    whole, in_spec, out_spec, pre_spec = layer_specs(layer, rows, width)
    bf16_rows = jax.ShapeDtypeStruct((rows, width), jnp.bfloat16)
    last = scale is not None
    return pl.pallas_call(
        functools.partial(forward_body, scale, 4),
        grid=(ff // FF_TILE,),
        out_shape=[jax.ShapeDtypeStruct((rows, ff), jnp.bfloat16), bf16_rows] if last else bf16_rows,
        in_specs=[whole, in_spec, out_spec] + ([whole] if last else []),
        out_specs=[pre_spec, whole] if last else whole,
        scratch_shapes=[pltpu.VMEM((rows, width), jnp.float32)],
        name="layer_forward",
        **layer_params(rows, width, ff),
    )(*((hidden, w_in, w_out) + ((target,) if last else ())))


def backward_body(parts, grad, pre, w_in, w_out, out, acc):
    step = pl.program_id(0)
    rows = grad.shape[0] // parts

    @pl.when(step == 0)
    def _():
        acc[...] = grad[...].astype(jnp.float32)

    for part in range(parts):
        at = pl.ds(part * rows, rows)
        e = rounded(dot_nt(grad[at], w_out[0]))
        slope = gelu_parts(pre[at].astype(jnp.float32))[1]
        acc[at] += dot_nt((slope * e).astype(jnp.bfloat16), w_in[0])

    @pl.when(step == pl.num_programs(0) - 1)
    def _():
        out[...] = acc[...].astype(jnp.bfloat16)


def layer_backward(grad, pre, w_in, w_out, layer):
    (rows, width), ff = grad.shape, w_in.shape[2]
    whole, in_spec, out_spec, pre_spec = layer_specs(layer, rows, width)
    return pl.pallas_call(
        functools.partial(backward_body, 4),
        grid=(ff // FF_TILE,),
        out_shape=jax.ShapeDtypeStruct((rows, width), jnp.bfloat16),
        in_specs=[whole, pre_spec, in_spec, out_spec],
        out_specs=whole,
        scratch_shapes=[pltpu.VMEM((rows, width), jnp.float32)],
        name="layer_backward",
        **layer_params(rows, width, ff),
    )(grad, pre, w_in, w_out)


def grads_body(count, tile, layer, bits, parts, split, *refs):
    hidden, grad = refs[:count], refs[count : 2 * count]
    w_in, w_out, out_a, out_b, hidden_buf, grad_buf, act_buf, pre_buf, window, w_in_t, w_out_buf, sem, w_sem = refs[2 * count :]
    block, width = w_in_t.shape
    span = window.shape[1]
    step, steps = pl.program_id(0), pl.num_programs(0)
    per = hidden[0].shape[0] // tile
    owner = lax.axis_index(AXIS) ^ bits
    start = jnp.minimum(owner * block // 128 * 128, w_in.shape[2] - span)
    in_copy = pltpu.make_async_copy(w_in.at[layer, :, pl.ds(pl.multiple_of(start, 128), span)], window, w_sem.at[0])
    out_copy = pltpu.make_async_copy(w_out.at[layer, pl.ds(pl.multiple_of(owner * block, 16), block)], w_out_buf, w_sem.at[1])

    def fetch(at, slot):
        for b in range(count):
            @pl.when(at // per == b)
            def _():
                rows = pl.ds(pl.multiple_of((at % per) * tile, tile), tile)
                pltpu.make_async_copy(hidden[b].at[rows], hidden_buf.at[slot], sem.at[0, slot]).start()
                pltpu.make_async_copy(grad[b].at[rows], grad_buf.at[slot], sem.at[1, slot]).start()

    slot = step % 2

    @pl.when(step == 0)
    def _():
        in_copy.start()
        out_copy.start()
        fetch(0, 0)
        in_copy.wait()
        chosen = lax.broadcasted_iota(jnp.int32, (block, span), 0) + (owner * block - start)
        chosen = (chosen == lax.broadcasted_iota(jnp.int32, (block, span), 1)).astype(jnp.bfloat16)
        w_in_t[...] = dot_nt(chosen, window[...]).astype(jnp.bfloat16)
        out_copy.wait()

    @pl.when(step + 1 < steps)
    def _():
        fetch(step + 1, 1 - slot)

    pltpu.make_async_copy(hidden[0].at[pl.ds(0, tile)], hidden_buf.at[slot], sem.at[0, slot]).wait()
    pltpu.make_async_copy(grad[0].at[pl.ds(0, tile)], grad_buf.at[slot], sem.at[1, slot]).wait()

    rows = tile // parts
    for part in range(parts):
        at = pl.ds(part * rows, rows)
        u = rounded(dot_nt(w_in_t[...], hidden_buf[slot, at]))
        e = rounded(dot_nt(w_out_buf[...], grad_buf[slot, at]))
        act, slope = gelu_parts(u)
        act_buf[:, at] = act.astype(jnp.bfloat16)
        pre_buf[:, at] = (slope * e).astype(jnp.bfloat16)
    second = dot_nn(act_buf[...], grad_buf[slot])
    first = dot_nn(pre_buf[...], hidden_buf[slot])

    half = width // 2
    pieces = (
        [(out_a, (0,), second[:, :half]), (out_b, (0,), second[:, half:]), (out_a, (1,), first[:, :half]), (out_b, (1,), first[:, half:])]
        if split
        else [(out_a, (), second), (out_b, (), first)]
    )

    @pl.when(step == 0)
    def _():
        for ref, at, value in pieces:
            ref[at + (...,)] = value

    @pl.when(step > 0)
    def _():
        for ref, at, value in pieces:
            ref[at + (...,)] += value


def column_grads(hidden, grad, w_in, w_out, layer, bits, split):
    count, width = len(hidden), hidden[0].shape[1]
    block = w_in.shape[2] // DEVICES
    span = -(-(block + 128) // 128) * 128
    tokens = count * hidden[0].shape[0]
    tile = 1024
    shape = (2, block, width // 2) if split else (block, width)
    spec = pl.BlockSpec(shape, lambda t: (0,) * len(shape))
    bf16 = jnp.bfloat16
    return pl.pallas_call(
        functools.partial(grads_body, count, tile, layer, bits, 2, split),
        grid=(tokens // tile,),
        out_shape=[jax.ShapeDtypeStruct(shape, jnp.float32)] * 2,
        in_specs=[pl.BlockSpec(memory_space=pl.ANY)] * (2 * count + 2),
        out_specs=[spec, spec],
        scratch_shapes=[pltpu.VMEM((2, tile, width), bf16)] * 2
        + [pltpu.VMEM((block, tile), bf16)] * 2
        + [pltpu.VMEM((width, span), bf16), pltpu.VMEM((block, width), bf16), pltpu.VMEM((block, width), bf16)]
        + [pltpu.SemaphoreType.DMA((2, 2)), pltpu.SemaphoreType.DMA((2,))],
        compiler_params=pltpu.CompilerParams(vmem_limit_bytes=62 * 2**20, dimension_semantics=("arbitrary",)),
        cost_estimate=pl.CostEstimate(
            flops=8 * tokens * block * width,
            bytes_accessed=4 * tokens * width + 12 * block * width,
            transcendentals=tokens * block,
        ),
        name="column_grads",
    )(*hidden, *grad, w_in, w_out)


def into_layer(body, inputs, in_specs, spec_of, grid, layer, shape, held):
    extra = [] if held is None else [held]
    return pl.pallas_call(
        functools.partial(body, len(inputs)),
        grid=grid,
        out_shape=jax.ShapeDtypeStruct(shape, jnp.float32),
        in_specs=in_specs + [pl.BlockSpec(memory_space=pl.ANY)] * len(extra),
        out_specs=spec_of(layer),
        input_output_aliases={len(inputs): 0} if extra else {},
        compiler_params=pltpu.CompilerParams(vmem_limit_bytes=48 * 2**20, dimension_semantics=("arbitrary",)),
    )(*inputs, *extra)


def sum_body(count, *refs):
    total = refs[0][...]
    for ref in refs[1:count]:
        total = total + ref[...]
    refs[-1][0] = total


def sum_into(parts, layer, layers, held):
    block, width = parts[0].shape
    rows = block // 5
    spec = pl.BlockSpec((rows, width), lambda i: (i, 0))
    return into_layer(sum_body, parts, [spec] * len(parts), lambda layer: pl.BlockSpec((1, rows, width), lambda i: (layer, i, 0)), (5,), layer, (layers, block, width), held)


def sum_halves_body(count, *refs):
    half = refs[0].shape[2]
    for side in range(2):
        mine = refs[side:count:2]
        total = mine[0][0]
        for ref in mine[1:]:
            total = total + ref[0]
        refs[-1][0, :, side * half : (side + 1) * half] = total


def sum_halves_into(pairs, layer, layers, held):
    _, block, half = pairs[0][0].shape
    rows = block // 5
    flat = [part for pair in pairs for part in pair]
    spec = pl.BlockSpec((1, rows, half), lambda i: (0, i, 0))
    return into_layer(sum_halves_body, flat, [spec] * len(flat), lambda layer: pl.BlockSpec((1, rows, 2 * half), lambda i: (layer, i, 0)), (5,), layer, (layers, block, 2 * half), held)


def turn_body(layer0, *refs):
    out = refs[-1]
    block = refs[0].shape[-2]
    for side in range(2):
        total = refs[side][...]
        for ref in refs[2 + side : layer0 : 2]:
            total = total + ref[...]
        out[side, :, :block] = total.T
        total = refs[layer0 + side][0]
        for ref in refs[layer0 + 2 + side : -1 : 2]:
            total = total + ref[0]
        out[side, :, block:] = total.T


def turn(layer0, layer1):
    block, width = layer0[0].shape
    half, step = width // 2, 256
    blocks = half // step
    low = pl.BlockSpec((block, step), lambda j: (0, j))
    high = pl.BlockSpec((block, step), lambda j: (0, blocks + j))
    part = pl.BlockSpec((1, block, step), lambda j: (1, 0, j))
    flat0 = [array for array in layer0 for _ in range(2)]
    flat1 = [array for pair in layer1 for array in pair]
    out = pl.pallas_call(
        functools.partial(turn_body, len(flat0)),
        grid=(blocks,),
        out_shape=jax.ShapeDtypeStruct((2, half, 2 * block), jnp.float32),
        in_specs=[low, high] * len(layer0) + [part] * len(flat1),
        out_specs=pl.BlockSpec((2, step, 2 * block), lambda j: (0, j, 0)),
        compiler_params=pltpu.CompilerParams(vmem_limit_bytes=48 * 2**20, dimension_semantics=("arbitrary",)),
        name="turn",
    )(*flat0, *flat1)
    return out.reshape(DEVICES, width // DEVICES, 2 * block)


def join_body(blocks, out):
    block = blocks.shape[2] // 2
    for layer in range(2):
        for i in range(blocks.shape[0]):
            out[layer, :, i * block : (i + 1) * block] = blocks[i, :, layer * block : (layer + 1) * block]


def join(blocks):
    count, rows, both = blocks.shape
    step = 32
    return pl.pallas_call(
        join_body,
        grid=(rows // step,),
        out_shape=jax.ShapeDtypeStruct((2, rows, count * both // 2), jnp.float32),
        in_specs=[pl.BlockSpec((count, step, both), lambda i: (0, i, 0))],
        out_specs=pl.BlockSpec((2, step, count * both // 2), lambda i: (0, i, 0)),
        compiler_params=pltpu.CompilerParams(vmem_limit_bytes=48 * 2**20, dimension_semantics=("arbitrary",)),
        name="join",
    )(blocks)


def solution(mesh):
    def local_grads(tokens, targets, w_in, w_out):
        layers = w_in.shape[0]
        scale = (tokens.shape[0] * DEVICES) ** -0.5

        def gather_plane(value):
            return lax.all_gather(value, AXIS, axis_index_groups=groups_of(CORE | Y | Z), tiled=True)

        def gather_pair(value):
            across = swap(value, X)
            near = swap(value, CORE)
            return [value, near, across, swap(across, CORE)]

        all_tokens = gather_plane(tokens)
        hidden1 = layer_forward(tokens, w_in, w_out, 0)
        hidden1_all = gather_pair(hidden1)
        pre1, grad1 = layer_forward(hidden1, w_in, w_out, 1, targets, scale)
        grad1_all = gather_pair(grad1)
        grad0 = layer_backward(grad1, pre1, w_in, w_out, 1)
        all_grad0 = gather_plane(grad0)

        def columns(hidden, grad, layer, bits, split):
            return column_grads(hidden, grad, w_in, w_out, layer, bits, split)

        own1 = columns(hidden1_all, grad1_all, 1, 0, True)
        far_lo, far_hi = columns(hidden1_all, grad1_all, 1, Y | Z, True)
        far_lo = swap(far_lo, Y)
        far_hi = swap(far_hi, Z)
        y_lo, y_hi = columns(hidden1_all, grad1_all, 1, Y, True)
        y_lo = swap(y_lo, Y)
        z_lo, z_hi = columns(hidden1_all, grad1_all, 1, Z, True)
        z_hi = swap(z_hi, Z)
        second0_x, first0_x = columns([all_tokens], [all_grad0], 0, X, False)
        first0_x = swap(first0_x, X)
        second0_x = swap(second0_x, X)
        y_hi = swap(y_hi + far_hi, Y)
        z_lo = swap(z_lo + far_lo, Z)
        second0, first0 = columns([all_tokens], [all_grad0], 0, 0, False)

        rows = turn([first0, first0_x], [own1, (y_lo, y_hi), (z_lo, z_hi)])
        rows = lax.all_to_all(rows, AXIS, split_axis=0, concat_axis=0, tiled=True)
        out_second = sum_halves_into([own1, (y_lo, y_hi), (z_lo, z_hi)], 1, layers, None)
        out_second = sum_into([second0, second0_x], 0, layers, out_second)
        out_first = join(rows)
        return out_first, out_second

    tok_spec = P(AXIS, None)
    grad_spec = P(None, AXIS, None)
    return jax.shard_map(local_grads, mesh=mesh, in_specs=(tok_spec, tok_spec, P(), P()), out_specs=(grad_spec, grad_spec), check_vma=False)
```

time: 1350 us -> 910 us (0.67)
  Pallas kernels: 0 us -> 538 us
  waiting for transfers between devices: 787 us -> 312 us
  matrix products: 452 us -> 0 us
  local copies, waits for them, and re-layouts: 80.5 us -> 10.6 us
  starting transfers between devices: 0.16 us -> 19.1 us
    pallas_call x0 -> x13, Pallas kernels: none -> 538 us  [the longest x6 300 us: column_grads(): pl.pallas_call(functools.partial(grads_body, count, tile, layer, bits, 2,...]
    reduce_scatter x2 -> x0, waiting for transfers between devices: 523 us -> none  [local_grads(): lax.psum_scatter(grad_second, 'data', scatter_dimension=0, tiled=True)]
    dot_general x10 -> x0, matrix products: 416 us -> none  [the longest x2 110 us: local_grads(): jnp.einsum('td,fd->tf', grad_h, w_out[layer], preferred_element_type=jnp....]
    ppermute x0 -> x14, waiting for transfers between devices: none -> 311 us  [swap(): return lax.ppermute(value, AXIS, [(i, i ^ bits) for i in range(DEVICES)])]
    unnamed x6 -> x2, waiting for transfers between devices: 263 us -> 0.7 us
    unnamed x16 -> x20, local copies, waits for them, and re-layouts: 80.5 us -> 10.6 us
    unnamed x1 -> x0, matrix products: 35.8 us -> none
    ppermute x0 -> x14, starting transfers between devices: none -> 15.2 us  [swap(): return lax.ppermute(value, AXIS, [(i, i ^ bits) for i in range(DEVICES)])]
  transfers between devices with their start and end apart: 4 -> 17, of which waited for: 3 -> 6; matrix products, arithmetic and copies ran while one was open for 22% -> 1% of each run, Pallas kernels for 0% -> 58%
where the time goes in v1:
time: 910 us; the launch traced here: 903 us
  Pallas kernels  538 us (59%)
  waiting for transfers between devices  312 us (34%)
  starting transfers between devices  19.1 us (2%)
  between operations  14.5 us (2%)
  local copies, waits for them, and re-layouts  10.6 us (1%)
  other arithmetic  9.5 us (1%)
    ppermute x14, waiting for transfers between devices, swap(): return lax.ppermute(value, AXIS, [(i, i ^ bits) for i in range(DEVICES)])  311 us
    pallas_call x6, Pallas kernels, column_grads(): pl.pallas_call(functools.partial(grads_body, count, tile, layer, bits, 2,...  300 us
    pallas_call x2, Pallas kernels, layer_forward(): pl.pallas_call(functools.partial(forward_body, scale, 4), grid=(ff // FF_...  138 us
    pallas_call x1, Pallas kernels, layer_backward(): pl.pallas_call(functools.partial(backward_body, 4), grid=(ff // FF_TILE,)...  70.1 us
  transfers between devices with their start and end apart: 17, of which 6 were waited for; matrix products, arithmetic and copies ran while one was open for 1% of the time, Pallas kernels for 58%

profile of v1, /device:TPU:0, one launch (start us, length us, event | category | flops | bytes accessed | tf_op | source)
XLA Modules:
  0.0 903.5 jit_solution(9971549187397876072)
XLA Ops:
  7.9 67.3 %layer_forward.2.refs_0_ = bf16[1024,1536]{1,0:T(8,128)(2,1)} custom-call(bf16[1024,1536]{1,0:T(8,128)(2,1)} %refs_0_.1, bf16[2,1536,8960]{2,1,0:T(8,128)(2,1)} %refs_8_.7, bf16[2,8960,1536]{2,1,0:T(8,128)(2,1)} %refs_9_.7), custom_call_target="tpu_custom_call" | custom-call | flops 56371445760 | bytes 55050240 | tf_op jit(solution)/shard_map/layer_forward/pallas_call | solution.py:101
  75.2 70.6 %layer_forward.3 = (bf16[1024,8960]{1,0:T(8,128)(2,1)}, bf16[1024,1536]{1,0:T(8,128)(2,1)}) custom-call(bf16[1024,1536]{1,0:T(8,128)(2,1)} %layer_forward.2.refs_0_, bf16[2,1536,8960]{2,1,0:T(8,128)(2,1)} %refs_8_.7, bf16[2,8960,1536]{2,1,0:T(8,128)(2,1)} %refs_9_.7, bf16[1024,1536]{1,0:T(8,128)(2,1)} %refs_3_.3), custom_call_target="tpu_custom_call" | custom-call | flops 56371445760 | bytes 55050240 | tf_op jit(solution)/shard_map/layer_forward/pallas_call | solution.py:101
  145.8 70.1 %layer_backward.1 = bf16[1024,1536]{1,0:T(8,128)(2,1)} custom-call(bf16[1024,1536]{1,0:T(8,128)(2,1)} %get-tuple-element.16.grad.refs_4_, bf16[1024,8960]{1,0:T(8,128)(2,1)} %get-tuple-element.17.pre, bf16[2,1536,8960]{2,1,0:T(8,128)(2,1)} %refs_8_.7, bf16[2,8960,1536]{2,1,0:T(8,128)(2,1)} %refs_9_.7), custom_call_target="tpu_custom_call" | custom-call | flops 56371445760 | bytes 55050240 | tf_op jit(solution)/shard_map/layer_backward/pallas_call | solution.py:135
  215.9 3.6 collective-permute-start.2
  220.0 68.6 %collective-permute-done.2.refs_2_ = bf16[1024,1536]{1,0:T(8,128)(2,1)S(1)} collective-permute-done((bf16[1024,1536]{1,0:T(8,128)(2,1)}, bf16[1024,1536]{1,0:T(8,128)(2,1)S(1)}, u32[]{:S(2)}, u32[]{:S(2)}) %collective-permute-start.2) | collective-permute-done | bytes 3145760 | tf_op jit(solution)/shard_map/ppermute | solution.py:27
  290.3 64.9 %collective-permute-done.5.refs_6_ = bf16[1024,1536]{1,0:T(8,128)(2,1)S(1)} collective-permute-done((bf16[1024,1536]{1,0:T(8,128)(2,1)}, bf16[1024,1536]{1,0:T(8,128)(2,1)S(1)}, u32[]{:S(2)}, u32[]{:S(2)}) %collective-permute-start.5) | collective-permute-done | bytes 3145760 | tf_op jit(solution)/shard_map/ppermute | solution.py:27
  361.0 39.3 %column_grads.9 = (f32[2,560,768]{2,1,0:T(8,128)}, f32[2,560,768]{2,1,0:T(8,128)}) custom-call(bf16[1024,1536]{1,0:T(8,128)(2,1)} %layer_forward.2.refs_0_, bf16[1024,1536]{1,0:T(8,128)(2,1)} %copy-done.5, bf16[1024,1536]{1,0:T(8,128)(2,1)} %copy-done.3, bf16[1024,1536]{1,0:T(8,128)(2,1)} %copy-done.7, bf16[1024,1536]{1,0:T(8,128)(2,1)} %get-tuple-element.16.grad.refs_4_, ...), custom_call_target="tpu_custom_call" | custom-call | flops 28185722880 | bytes 35487744 | tf_op jit(solution)/shard_map/column_grads/pallas_call | solution.py:225
  400.4 1.8 collective-permute-start.7
  402.2 39.3 %column_grads.10 = (f32[2,560,768]{2,1,0:T(8,128)}, f32[2,560,768]{2,1,0:T(8,128)}) custom-call(bf16[1024,1536]{1,0:T(8,128)(2,1)} %layer_forward.2.refs_0_, bf16[1024,1536]{1,0:T(8,128)(2,1)} %copy-done.5, bf16[1024,1536]{1,0:T(8,128)(2,1)} %copy-done.3, bf16[1024,1536]{1,0:T(8,128)(2,1)} %copy-done.7, bf16[1024,1536]{1,0:T(8,128)(2,1)} %get-tuple-element.16.grad.refs_4_, ...), custom_call_target="tpu_custom_call" | custom-call | flops 28185722880 | bytes 35487744 | tf_op jit(solution)/shard_map/column_grads/pallas_call | solution.py:225
  443.6 39.5 %column_grads.11 = (f32[2,560,768]{2,1,0:T(8,128)}, f32[2,560,768]{2,1,0:T(8,128)}) custom-call(bf16[1024,1536]{1,0:T(8,128)(2,1)} %layer_forward.2.refs_0_, bf16[1024,1536]{1,0:T(8,128)(2,1)} %copy-done.5, bf16[1024,1536]{1,0:T(8,128)(2,1)} %copy-done.3, bf16[1024,1536]{1,0:T(8,128)(2,1)} %copy-done.7, bf16[1024,1536]{1,0:T(8,128)(2,1)} %get-tuple-element.16.grad.refs_4_, ...), custom_call_target="tpu_custom_call" | custom-call | flops 28185722880 | bytes 35487744 | tf_op jit(solution)/shard_map/column_grads/pallas_call | solution.py:225
  483.4 39.3 %column_grads.8 = (f32[2,560,768]{2,1,0:T(8,128)}, f32[2,560,768]{2,1,0:T(8,128)}) custom-call(bf16[1024,1536]{1,0:T(8,128)(2,1)} %layer_forward.2.refs_0_, bf16[1024,1536]{1,0:T(8,128)(2,1)} %copy-done.5, bf16[1024,1536]{1,0:T(8,128)(2,1)} %copy-done.3, bf16[1024,1536]{1,0:T(8,128)(2,1)} %copy-done.7, bf16[1024,1536]{1,0:T(8,128)(2,1)} %get-tuple-element.16.grad.refs_4_, ...), custom_call_target="tpu_custom_call" | custom-call | flops 28185722880 | bytes 35487744 | tf_op jit(solution)/shard_map/column_grads/pallas_call | solution.py:225
  522.7 5.4 add.6
  529.8 21.9 %collective-permute-done.10 = f32[2,560,768]{2,1,0:T(8,128)} collective-permute-done((f32[2,560,768]{2,1,0:T(8,128)}, f32[2,560,768]{2,1,0:T(8,128)}, u32[]{:S(2)}, u32[]{:S(2)}) %collective-permute-start.10) | collective-permute-done | bytes 3440672 | tf_op jit(solution)/shard_map/ppermute | solution.py:27
  551.8 4.2 add.7
  555.9 1.8 collective-permute-start.11
  557.7 71.4 %column_grads.7 = (f32[560,1536]{1,0:T(8,128)}, f32[560,1536]{1,0:T(8,128)}) custom-call(bf16[8192,1536]{1,0:T(8,128)(2,1)} %all-gather.3.cloned.1.call-done.refs_0_, bf16[8192,1536]{1,0:T(8,128)(2,1)} %all-gather.5.cloned.1.call-done.refs_1_, bf16[2,1536,8960]{2,1,0:T(8,128)(2,1)} %refs_8_.7, bf16[2,8960,1536]{2,1,0:T(8,128)(2,1)} %refs_9_.7), custom_call_target="tpu_custom_call" | custom-call | flops 56371445760 | bytes 60653568 | tf_op jit(solution)/shard_map/column_grads/pallas_call | solution.py:225
  630.7 71.6 %column_grads.6 = (f32[560,1536]{1,0:T(8,128)}, f32[560,1536]{1,0:T(8,128)}) custom-call(bf16[8192,1536]{1,0:T(8,128)(2,1)} %all-gather.3.cloned.1.call-done.refs_0_, bf16[8192,1536]{1,0:T(8,128)(2,1)} %all-gather.5.cloned.1.call-done.refs_1_, bf16[2,1536,8960]{2,1,0:T(8,128)(2,1)} %refs_8_.7, bf16[2,8960,1536]{2,1,0:T(8,128)(2,1)} %refs_9_.7), custom_call_target="tpu_custom_call" | custom-call | flops 56371445760 | bytes 60653568 | tf_op jit(solution)/shard_map/column_grads/pallas_call | solution.py:225
  704.0 2.0 copy-done
  706.0 10.1 %turn.1 = f32[2,768,1120]{2,1,0:T(8,128)} custom-call(f32[560,1536]{1,0:T(8,128)S(1)} %copy-done, f32[560,1536]{1,0:T(8,128)S(1)} %copy-done, f32[560,1536]{1,0:T(8,128)} %collective-permute-done.refs_2_.refs_3_, f32[560,1536]{1,0:T(8,128)} %collective-permute-done.refs_2_.refs_3_, f32[2,560,768]{2,1,0:T(8,128)} %get-tuple-element.20.refs_4_.refs_0_, ...), custom_call_target="tpu_custom_call" | custom-call | tf_op jit(solution)/shard_map/turn/pallas_call | solution.py:313
  716.1 3.8 all-to-all-start
  721.7 6.6 shard_map.59.refs_2_
  728.2 153.2 %collective-permute-done.13.refs_1_ = f32[560,1536]{1,0:T(8,128)S(1)} collective-permute-done((f32[560,1536]{1,0:T(8,128)}, f32[560,1536]{1,0:T(8,128)S(1)}, u32[]{:S(2)}, u32[]{:S(2)}) %collective-permute-start.13) | collective-permute-done | bytes 3440672 | tf_op jit(solution)/shard_map/ppermute | solution.py:27
  883.2 5.5 shard_map.60
  888.6 7.7 join.1
  (47 shorter events, 19.6 us)
Async XLA Ops:
  7.2 550.6 %all-gather.3.cloned.1.call-start = ((), (), s32[]{:S(2)}) async-start(), calls=%async_computation.1 | async-start | bytes 28311552 | tf_op jit(solution)/shard_map/all_gather | solution.py:352
  7.9 549.8 %all-gather.5.cloned.1.call-start = ((), (), s32[]{:S(2)}) async-start(), calls=%async_computation.2 | async-start | bytes 28311552 | tf_op jit(solution)/shard_map/all_gather | solution.py:352
  215.9 72.7 %collective-permute-start.2 = (bf16[1024,1536]{1,0:T(8,128)(2,1)}, bf16[1024,1536]{1,0:T(8,128)(2,1)S(1)}, u32[]{:S(2)}, u32[]{:S(2)}) collective-permute-start(bf16[1024,1536]{1,0:T(8,128)(2,1)} %layer_forward.2.refs_0_), channel_id=1, source_target_pairs={{0,2},{1,3},{2,0},{3,1},{4,6},{5,7},{6,4},{7,5},{8,10},{9,11},{10,... | collective-permute-start | bytes 9437192 | tf_op jit(solution)/shard_map/ppermute | solution.py:27
  219.5 135.7 %collective-permute-start.5 = (bf16[1024,1536]{1,0:T(8,128)(2,1)}, bf16[1024,1536]{1,0:T(8,128)(2,1)S(1)}, u32[]{:S(2)}, u32[]{:S(2)}) collective-permute-start(bf16[1024,1536]{1,0:T(8,128)(2,1)} %get-tuple-element.16.grad.refs_4_), channel_id=1, source_target_pairs={{0,2},{1,3},{2,0},{3,1},{4,6},{5,7},{6,4},{7,5},{8,10},{9,11},{10,... | collective-permute-start | bytes 9437192 | tf_op jit(solution)/shard_map/ppermute | solution.py:27
  219.5 135.7 %collective-permute-start.1 = (bf16[1024,1536]{1,0:T(8,128)(2,1)}, bf16[1024,1536]{1,0:T(8,128)(2,1)S(1)}, u32[]{:S(2)}, u32[]{:S(2)}) collective-permute-start(bf16[1024,1536]{1,0:T(8,128)(2,1)} %layer_forward.2.refs_0_), channel_id=1, source_target_pairs={{0,1},{1,0},{2,3},{3,2},{4,5},{5,4},{6,7},{7,6},{8,9},{9,8},{10,11... | collective-permute-start | bytes 9437192 | tf_op jit(solution)/shard_map/ppermute | solution.py:27
  219.5 135.7 %collective-permute-start.4 = (bf16[1024,1536]{1,0:T(8,128)(2,1)}, bf16[1024,1536]{1,0:T(8,128)(2,1)S(1)}, u32[]{:S(2)}, u32[]{:S(2)}) collective-permute-start(bf16[1024,1536]{1,0:T(8,128)(2,1)} %get-tuple-element.16.grad.refs_4_), channel_id=1, source_target_pairs={{0,1},{1,0},{2,3},{3,2},{4,5},{5,4},{6,7},{7,6},{8,9},{9,8},{10,11... | collective-permute-start | bytes 9437192 | tf_op jit(solution)/shard_map/ppermute | solution.py:27
  290.3 65.0 %collective-permute-start.3 = (bf16[1024,1536]{1,0:T(8,128)(2,1)S(1)}, bf16[1024,1536]{1,0:T(8,128)(2,1)S(1)}, u32[]{:S(2)}, u32[]{:S(2)}) collective-permute-start(bf16[1024,1536]{1,0:T(8,128)(2,1)S(1)} %collective-permute-done.2.refs_2_), channel_id=1, source_target_pairs={{0,1},{1,0},{2,3},{3,2},{4,5},{5,4},{6,7},{7,6},{8,9},{9,8},{10,11... | collective-permute-start | bytes 9437192 | tf_op jit(solution)/shard_map/ppermute | solution.py:27
  355.2 5.8 collective-permute-start.6
  355.2 2.6 copy-start.5
  355.3 3.6 copy-start.6
  400.4 301.9 %collective-permute-start.7 = (f32[2,560,768]{2,1,0:T(8,128)}, f32[2,560,768]{2,1,0:T(8,128)}, u32[]{:S(2)}, u32[]{:S(2)}) collective-permute-start(f32[2,560,768]{2,1,0:T(8,128)} %get-tuple-element.22), channel_id=1, source_target_pairs={{0,4},{1,5},{2,6},{3,7},{4,0},{5,1},{6,2},{7,3},{8,12},{9,13},{10,... | collective-permute-start | bytes 10321928 | tf_op jit(solution)/shard_map/ppermute | solution.py:27
  441.5 81.1 %collective-permute-start.8 = (f32[2,560,768]{2,1,0:T(8,128)}, f32[2,560,768]{2,1,0:T(8,128)}, u32[]{:S(2)}, u32[]{:S(2)}) collective-permute-start(f32[2,560,768]{2,1,0:T(8,128)} %get-tuple-element.24), channel_id=1, source_target_pairs={{0,8},{1,9},{2,10},{3,11},{4,12},{5,13},{6,14},{7,15},{8,0},{9,1},... | collective-permute-start | bytes 10321928 | tf_op jit(solution)/shard_map/ppermute | solution.py:27
  443.1 108.6 %collective-permute-start.10 = (f32[2,560,768]{2,1,0:T(8,128)}, f32[2,560,768]{2,1,0:T(8,128)}, u32[]{:S(2)}, u32[]{:S(2)}) collective-permute-start(f32[2,560,768]{2,1,0:T(8,128)} %get-tuple-element.26), channel_id=1, source_target_pairs={{0,4},{1,5},{2,6},{3,7},{4,0},{5,1},{6,2},{7,3},{8,12},{9,13},{10,... | collective-permute-start | bytes 10321928 | tf_op jit(solution)/shard_map/ppermute | solution.py:27
  483.1 219.2 %collective-permute-start.12 = (f32[2,560,768]{2,1,0:T(8,128)}, f32[2,560,768]{2,1,0:T(8,128)}, u32[]{:S(2)}, u32[]{:S(2)}) collective-permute-start(f32[2,560,768]{2,1,0:T(8,128)} %get-tuple-element.27), channel_id=1, source_target_pairs={{0,8},{1,9},{2,10},{3,11},{4,12},{5,13},{6,14},{7,15},{8,0},{9,1},... | collective-permute-start | bytes 10321928 | tf_op jit(solution)/shard_map/ppermute | solution.py:27
  522.7 29.1 %copy-start.9 = (f32[2,560,768]{2,1,0:T(8,128)S(1)}, f32[2,560,768]{2,1,0:T(8,128)}, u32[]{:S(2)}) copy-start(f32[2,560,768]{2,1,0:T(8,128)} %get-tuple-element.25) | copy-start | bytes 10321924
  528.0 174.3 %collective-permute-start.9 = (f32[2,560,768]{2,1,0:T(8,128)}, f32[2,560,768]{2,1,0:T(8,128)}, u32[]{:S(2)}, u32[]{:S(2)}) collective-permute-start(f32[2,560,768]{2,1,0:T(8,128)} %add.6), channel_id=1, source_target_pairs={{0,4},{1,5},{2,6},{3,7},{4,0},{5,1},{6,2},{7,3},{8,12},{9,13},{10,... | collective-permute-start | bytes 10321928 | tf_op jit(solution)/shard_map/ppermute | solution.py:27
  555.9 146.4 %collective-permute-start.11 = (f32[2,560,768]{2,1,0:T(8,128)}, f32[2,560,768]{2,1,0:T(8,128)}, u32[]{:S(2)}, u32[]{:S(2)}) collective-permute-start(f32[2,560,768]{2,1,0:T(8,128)} %add.7), channel_id=1, source_target_pairs={{0,8},{1,9},{2,10},{3,11},{4,12},{5,13},{6,14},{7,15},{8,0},{9,1},... | collective-permute-start | bytes 10321928 | tf_op jit(solution)/shard_map/ppermute | solution.py:27
  629.2 74.8 %collective-permute-start = (f32[560,1536]{1,0:T(8,128)}, f32[560,1536]{1,0:T(8,128)}, u32[]{:S(2)}, u32[]{:S(2)}) collective-permute-start(f32[560,1536]{1,0:T(8,128)} %get-tuple-element.19), channel_id=1, source_target_pairs={{0,2},{1,3},{2,0},{3,1},{4,6},{5,7},{6,4},{7,5},{8,10},{9,11},{10,... | collective-permute-start | bytes 10321928 | tf_op jit(solution)/shard_map/ppermute | solution.py:27
  704.0 2.0 copy-start
  716.1 5.6 copy-start.1
  716.1 172.5 %all-to-all-start = ((f32[16,96,1120]{2,1,0:T(8,128)}), f32[16,96,1120]{2,1,0:T(8,128)}, u32[]{:S(2)}, u32[]{:S(2)}) async-start(f32[16,96,1120]{2,1,0:T(8,128)} %bitcast.1), calls=%async_computation | async-start | bytes 14155776 | tf_op jit(solution)/shard_map/all_to_all | solution.py:386
  719.9 163.3 %copy-start.2 = (f32[560,1536]{1,0:T(8,128)S(1)}, f32[560,1536]{1,0:T(8,128)}, u32[]{:S(2)}) copy-start(f32[560,1536]{1,0:T(8,128)} %get-tuple-element.28.refs_0_) | copy-start | bytes 10321924
  719.9 161.5 %collective-permute-start.13 = (f32[560,1536]{1,0:T(8,128)}, f32[560,1536]{1,0:T(8,128)S(1)}, u32[]{:S(2)}, u32[]{:S(2)}) collective-permute-start(f32[560,1536]{1,0:T(8,128)} %get-tuple-element.29), channel_id=1, source_target_pairs={{0,2},{1,3},{2,0},{3,1},{4,6},{5,7},{6,4},{7,5},{8,10},{9,11},{10,... | collective-permute-start | bytes 10321928 | tf_op jit(solution)/shard_map/ppermute | solution.py:27
  881.4 1.7 copy-start.8
  (3 other events, 5.0 us)
Sparse Core Ops, SparseCore 0:
  9.8 124.2 all-gather.2
  216.0 124.6 all-gather.4

commit v2 on v0

v2 whole, which is shorter than its diff:
```python
import functools

import jax
import jax.numpy as jnp
from jax import lax
from jax.experimental import pallas as pl
from jax.experimental.pallas import tpu as pltpu
from jax.sharding import PartitionSpec as P


AXIS = "data"
DEVICES = 16
CORE, X, Y, Z = 1, 2, 4, 8
GELU_S = 0.7978845608028654
GELU_C = 0.044715


def swap(value, bits):
    return lax.ppermute(value, AXIS, [(i, i ^ bits) for i in range(DEVICES)])


def gelu_parts(u):
    sq = u * u
    th = jnp.tanh(u * (GELU_S + (GELU_S * GELU_C) * sq))
    cdf = 0.5 + 0.5 * th
    slope = cdf + (0.5 * u) * (1.0 - th * th) * (GELU_S + (3.0 * GELU_S * GELU_C) * sq)
    return u * cdf, slope


def rounded(value):
    return value.astype(jnp.bfloat16).astype(jnp.float32)


def dot_nn(a, b):
    return jnp.dot(a, b, preferred_element_type=jnp.float32)


def dot_nt(a, b):
    return lax.dot_general(a, b, (((1,), (1,)), ((), ())), preferred_element_type=jnp.float32)


def flipped(index, bits):
    for bit in (CORE, X, Y, Z):
        if bits & bit:
            index = index + bit - 2 * bit * (index // bit % 2)
    return index


def plane_rank(index):
    return index // Z % 2 * 4 + index // Y % 2 * 2 + index % 2


def plane_gather(own, every, send_sem, recv_sem, own_sem):
    me = lax.axis_index(AXIS)
    half = own.shape[0] // 2
    low, high = pl.ds(0, half), pl.ds(half, half)
    count = iter(range(16))

    def remote(src, dst, bits):
        n = next(count)
        return pltpu.make_async_remote_copy(
            src_ref=src, dst_ref=dst, send_sem=send_sem.at[n], recv_sem=recv_sem.at[n], device_id=(flipped(me, bits),), device_id_type=pl.DeviceIdType.MESH
        )

    def slot(bits):
        return every.at[plane_rank(flipped(me, bits))]

    def barrier():
        ready = pltpu.get_barrier_semaphore()
        for bits in (CORE, Y, Z):
            pl.semaphore_signal(ready, inc=1, device_id=(flipped(me, bits),), device_id_type=pl.DeviceIdType.MESH)
        pl.semaphore_wait(ready, 3)

    keep = pltpu.make_async_copy(own, slot(0), own_sem.at[0])
    first = [remote(own, slot(0), bits) for bits in (Y, Z, CORE)]
    from_y, from_z, far = slot(Y), slot(Z), slot(Y | Z)
    second = [
        remote(from_y.at[low], from_y.at[low], Z),
        remote(from_z.at[high], from_z.at[high], Y),
        remote(from_y, from_y, CORE),
        remote(from_z, from_z, CORE),
    ]
    last = [remote(far.at[low], far.at[low], CORE), remote(far.at[high], far.at[high], CORE)]
    return barrier, keep, first, second, last


GATHER_SEMS = [pltpu.SemaphoreType.DMA((9,)), pltpu.SemaphoreType.DMA((9,)), pltpu.SemaphoreType.DMA((1,))]


def grads_body(plan, count, outs, tile, parts, turn_at, *refs):
    arrays = refs[:count]
    w_in, w_out = refs[count : count + 2]
    own_block = arrays[-1]
    outputs = refs[count + 2 : count + 2 + outs]
    hidden_buf, grad_buf, act_buf, pre_buf, window, w_in_t, w_out_buf, acc, sem, w_sem, out_sem = refs[count + 2 + outs : count + 13 + outs]
    gather_sems = refs[count + 13 + outs :]
    block, width = w_in_t.shape
    span = window.shape[1]
    step, steps = pl.program_id(0), pl.num_programs(0)
    me = lax.axis_index(AXIS)

    begins, sources, at = [], [], 0
    for segment in plan:
        begins.append(at)
        for h, g in zip(segment["hidden"], segment["grad"]):
            tiles = arrays[h].shape[0] // tile
            sources.append((at, at + tiles, arrays[h], arrays[g]))
            at += tiles
    ends = begins[1:] + [at]
    index = sum([(step >= begin).astype(jnp.int32) for begin in begins[1:]], jnp.int32(0))
    side = index % 2
    fresh = step == begins[0]
    for begin in begins[1:]:
        fresh = fresh | (step == begin)

    def fetch(at, slot):
        for begin, end, hidden, grad in sources:
            @pl.when((at >= begin) & (at < end))
            def _():
                rows = pl.ds(pl.multiple_of((at - begin) * tile, tile), tile)
                pltpu.make_async_copy(hidden.at[rows], hidden_buf.at[slot], sem.at[0, slot]).start()
                pltpu.make_async_copy(grad.at[rows], grad_buf.at[slot], sem.at[1, slot]).start()

    def weights(k):
        segment = plan[k]
        owner = flipped(me, segment["bits"])
        start = jnp.minimum(owner * block // 128 * 128, w_in.shape[2] - span)
        return owner * block - start, (
            pltpu.make_async_copy(w_in.at[segment["layer"], :, pl.ds(pl.multiple_of(start, 128), span)], window, w_sem.at[0]),
            pltpu.make_async_copy(w_out.at[segment["layer"], pl.ds(pl.multiple_of(owner * block, 16), block)], w_out_buf.at[k % 2], w_sem.at[1]),
        )

    def results(k, which):
        out_a, out_b = outputs[2 * k : 2 * k + 2]
        if plan[k]["split"]:
            half = width // 2
            return [
                pltpu.make_async_copy(acc.at[k % 2, which, :, pl.ds(0, half)], out_a.at[which], out_sem.at[k % 2, 2 * which]),
                pltpu.make_async_copy(acc.at[k % 2, which, :, pl.ds(half, half)], out_b.at[which], out_sem.at[k % 2, 2 * which + 1]),
            ]
        return [pltpu.make_async_copy(acc.at[k % 2, which], (out_a, out_b)[which], out_sem.at[k % 2, 2 * which])]

    slot = step % 2

    @pl.when(step == 0)
    def _():
        for copy in weights(0)[1]:
            copy.start()
        fetch(0, 0)

    if turn_at is not None:
        barrier, keep, first, second, last = plane_gather(own_block, outputs[-1], *gather_sems)

        @pl.when(step == 0)
        def _():
            barrier()
            for copy in first + [keep]:
                copy.start()

        @pl.when(step == turn_at)
        def _():
            for copy in first[:2]:
                copy.wait_recv()
            for copy in second:
                copy.start()

    for k, begin in enumerate(begins):
        @pl.when(step == begin)
        def _(k=k):
            shift, copies = weights(k)
            copies[0].wait()
            chosen = lax.broadcasted_iota(jnp.int32, (block, span), 0) + shift
            chosen = (chosen == lax.broadcasted_iota(jnp.int32, (block, span), 1)).astype(jnp.bfloat16)
            w_in_t[...] = dot_nt(chosen, window[...]).astype(jnp.bfloat16)
            copies[1].wait()
            if k >= 2:
                for copy in results(k - 2, 0) + results(k - 2, 1):
                    copy.wait()

    for k, end in enumerate(ends[:-1]):
        @pl.when(step == end - 1)
        def _(k=k):
            for copy in weights(k + 1)[1]:
                copy.start()

    @pl.when(step + 1 < steps)
    def _():
        fetch(step + 1, 1 - slot)

    pltpu.make_async_copy(arrays[0].at[pl.ds(0, tile)], hidden_buf.at[slot], sem.at[0, slot]).wait()
    pltpu.make_async_copy(arrays[0].at[pl.ds(0, tile)], grad_buf.at[slot], sem.at[1, slot]).wait()

    rows = tile // parts
    for part in range(parts):
        at = pl.ds(part * rows, rows)
        u = rounded(dot_nt(w_in_t[...], hidden_buf[slot, at]))
        e = rounded(dot_nt(w_out_buf[side], grad_buf[slot, at]))
        act, slope = gelu_parts(u)
        act_buf[:, at] = act.astype(jnp.bfloat16)
        pre_buf[:, at] = (slope * e).astype(jnp.bfloat16)

    for which, left, right in ((0, act_buf, grad_buf), (1, pre_buf, hidden_buf)):
        value = dot_nn(left[...], right[slot])

        @pl.when(fresh)
        def _():
            acc[side, which] = value

        @pl.when(jnp.logical_not(fresh))
        def _():
            acc[side, which] += value

        for k, end in enumerate(ends):
            @pl.when(step == end - 1)
            def _(k=k):
                for copy in results(k, which):
                    copy.start()

    @pl.when(step == steps - 1)
    def _():
        if turn_at is not None:
            for copy in second[:2]:
                copy.wait_recv()
            for copy in last:
                copy.start()
            keep.wait()
            first[2].wait_recv()
            for copy in second[2:] + last:
                copy.wait_recv()
            for copy in first + second + last:
                copy.wait_send()
        for k in range(max(0, len(plan) - 2), len(plan)):
            for copy in results(k, 0) + results(k, 1):
                copy.wait()


def column_grads(segments, w_in, w_out, gathered=None, turn_at=None, collective_id=None):
    arrays, plan = [], []

    def place(array):
        for n, other in enumerate(arrays):
            if other is array:
                return n
        arrays.append(array)
        return len(arrays) - 1

    for hidden, grad, layer, bits, split in segments:
        plan.append(dict(hidden=[place(a) for a in hidden], grad=[place(a) for a in grad], layer=layer, bits=bits, split=split))
    width = arrays[0].shape[1]
    block = w_in.shape[2] // DEVICES
    span = -(-(block + 128) // 128) * 128
    tile = 1024
    tokens = sum(arrays[h].shape[0] for segment in plan for h in segment["hidden"])
    shapes = [(2, block, width // 2) if segment["split"] else (block, width) for segment in plan for _ in range(2)]
    out_shape = [jax.ShapeDtypeStruct(shape, jnp.float32) for shape in shapes]
    bf16 = jnp.bfloat16
    params = {}
    if gathered is not None:
        arrays.append(gathered)
        out_shape.append(jax.ShapeDtypeStruct((8,) + gathered.shape, bf16))
        params = dict(collective_id=collective_id, has_side_effects=True)
    hbm = pl.BlockSpec(memory_space=pl.ANY)
    return pl.pallas_call(
        functools.partial(grads_body, plan, len(arrays), len(out_shape), tile, 2, turn_at),
        grid=(tokens // tile,),
        out_shape=out_shape,
        in_specs=[hbm] * (len(arrays) + 2),
        out_specs=[hbm] * len(out_shape),
        scratch_shapes=[pltpu.VMEM((2, tile, width), bf16)] * 2
        + [pltpu.VMEM((block, tile), bf16)] * 2
        + [pltpu.VMEM((width, span), bf16), pltpu.VMEM((block, width), bf16), pltpu.VMEM((2, block, width), bf16)]
        + [pltpu.VMEM((2, 2, block, width), jnp.float32)]
        + [pltpu.SemaphoreType.DMA((2, 2)), pltpu.SemaphoreType.DMA((2,)), pltpu.SemaphoreType.DMA((2, 4))]
        + (GATHER_SEMS if gathered is not None else []),
        compiler_params=pltpu.CompilerParams(vmem_limit_bytes=62 * 2**20, dimension_semantics=("arbitrary",), **params),
        cost_estimate=pl.CostEstimate(
            flops=8 * tokens * block * width, bytes_accessed=4 * tokens * width + 12 * block * width * len(plan), transcendentals=tokens * block
        ),
        name="column_grads",
    )(*arrays, w_in, w_out)


FF_TILE = 1280


def pair_rank(index):
    return index // X % 2 * 2 + index % 2


def layers_body(scale, parts, tiles, *refs):
    tokens, targets, w_in, w_out, every, hidden_all, grad_all, below = refs[:8]
    now, target, acc, pre_buf, send_sem, recv_sem, own_sem, pair_send, pair_recv, local = refs[8:]
    step = pl.program_id(0)
    phase, tile = step // tiles, step % tiles
    me = lax.axis_index(AXIS)
    rows = now.shape[0] // parts
    _, keep, first, second, last = plane_gather(tokens, every, send_sem, recv_sem, own_sem)

    def remote(array, came, bits, n):
        place = array.at[pair_rank(flipped(me, came))]
        return pltpu.make_async_remote_copy(
            src_ref=place, dst_ref=place, send_sem=pair_send.at[n], recv_sem=pair_recv.at[n], device_id=(flipped(me, bits),), device_id_type=pl.DeviceIdType.MESH
        )

    def pair(array, n):
        store = pltpu.make_async_copy(now, array.at[pair_rank(me)], local.at[n])
        return store, remote(array, 0, X, 3 * n), remote(array, 0, CORE, 3 * n + 1), remote(array, X, CORE, 3 * n + 2)

    hidden_copies, grad_copies = pair(hidden_all, 0), pair(grad_all, 1)
    get_tokens = pltpu.make_async_copy(tokens, now, local.at[2])
    get_target = pltpu.make_async_copy(targets, target, local.at[3])
    put_below = pltpu.make_async_copy(now, below, local.at[4])

    def on(at):
        return pl.when(step == at)

    @on(0)
    def _():
        get_tokens.start()
        get_target.start()
        ready = pltpu.get_barrier_semaphore()
        for bits in (CORE, X, Y, Z):
            pl.semaphore_signal(ready, inc=1, device_id=(flipped(me, bits),), device_id_type=pl.DeviceIdType.MESH)
        pl.semaphore_wait(ready, 4)
        for copy in first + [keep]:
            copy.start()
        get_tokens.wait()

    @on(tiles)
    def _():
        hidden_copies[0].wait()
        hidden_copies[1].start()
        hidden_copies[2].start()

    @on(tiles + 1)
    def _():
        for copy in first[:2]:
            copy.wait_recv()
        for copy in second:
            copy.start()

    @on(2 * tiles - 1)
    def _():
        for copy in second[:2]:
            copy.wait_recv()
        for copy in last:
            copy.start()
        get_target.wait()

    @on(2 * tiles)
    def _():
        grad_copies[0].wait()
        grad_copies[1].start()
        grad_copies[2].start()
        hidden_copies[1].wait_recv()
        hidden_copies[3].start()

    @pl.when(tile == 0)
    def _():
        acc[...] = now[...].astype(jnp.float32)

    @pl.when(phase < 2)
    def _():
        for part in range(parts):
            at = pl.ds(part * rows, rows)
            pre = dot_nn(now[at], w_in[0]).astype(jnp.bfloat16)
            pre_buf[tile, at] = pre
            act = gelu_parts(pre.astype(jnp.float32))[0].astype(jnp.bfloat16)
            acc[at] += dot_nn(act, w_out[0])

    @pl.when(phase == 2)
    def _():
        for part in range(parts):
            at = pl.ds(part * rows, rows)
            e = rounded(dot_nt(now[at], w_out[0]))
            slope = gelu_parts(pre_buf[tile, at].astype(jnp.float32))[1]
            acc[at] += dot_nt((slope * e).astype(jnp.bfloat16), w_in[0])

    @on(tiles - 1)
    def _():
        now[...] = acc[...].astype(jnp.bfloat16)
        hidden_copies[0].start()

    @on(2 * tiles - 1)
    def _():
        now[...] = ((rounded(acc[...]) - target[...].astype(jnp.float32)) * scale).astype(jnp.bfloat16)
        grad_copies[0].start()

    @on(3 * tiles - 1)
    def _():
        now[...] = acc[...].astype(jnp.bfloat16)
        put_below.start()
        grad_copies[1].wait_recv()
        grad_copies[3].start()
        keep.wait()
        put_below.wait()
        first[2].wait_recv()
        for copy in second[2:] + last:
            copy.wait_recv()
        for copies in (hidden_copies, grad_copies):
            copies[2].wait_recv()
            copies[3].wait_recv()
            for copy in copies[1:]:
                copy.wait_send()
        for copy in first + second + last:
            copy.wait_send()


def run_layers(tokens, targets, w_in, w_out, scale, collective_id):
    (rows, width), ff = tokens.shape, w_in.shape[2]
    tiles = ff // FF_TILE
    bf16 = jnp.bfloat16
    hbm = pl.BlockSpec(memory_space=pl.ANY)
    return pl.pallas_call(
        functools.partial(layers_body, scale, 2, tiles),
        grid=(3 * tiles,),
        out_shape=[jax.ShapeDtypeStruct((n, rows, width), bf16) for n in (8, 4, 4)] + [jax.ShapeDtypeStruct((rows, width), bf16)],
        in_specs=[
            hbm,
            hbm,
            pl.BlockSpec((1, width, FF_TILE), lambda s: (jnp.minimum(s // tiles, 1), 0, s % tiles)),
            pl.BlockSpec((1, FF_TILE, width), lambda s: (jnp.minimum(s // tiles, 1), s % tiles, 0)),
        ],
        out_specs=[hbm] * 4,
        scratch_shapes=[
            pltpu.VMEM((rows, width), bf16),
            pltpu.VMEM((rows, width), bf16),
            pltpu.VMEM((rows, width), jnp.float32),
            pltpu.VMEM((tiles, rows, FF_TILE), bf16),
        ]
        + GATHER_SEMS
        + [pltpu.SemaphoreType.DMA((6,)), pltpu.SemaphoreType.DMA((6,)), pltpu.SemaphoreType.DMA((5,))],
        compiler_params=pltpu.CompilerParams(
            vmem_limit_bytes=62 * 2**20, dimension_semantics=("arbitrary",), collective_id=collective_id, has_side_effects=True
        ),
        cost_estimate=pl.CostEstimate(flops=12 * rows * width * ff, bytes_accessed=12 * width * ff, transcendentals=3 * rows * ff),
        name="run_layers",
    )(tokens, targets, w_in, w_out)


def into_layer(body, inputs, in_specs, spec_of, grid, layer, shape, held):
    extra = [] if held is None else [held]
    return pl.pallas_call(
        functools.partial(body, len(inputs)),
        grid=grid,
        out_shape=jax.ShapeDtypeStruct(shape, jnp.float32),
        in_specs=in_specs + [pl.BlockSpec(memory_space=pl.ANY)] * len(extra),
        out_specs=spec_of(layer),
        input_output_aliases={len(inputs): 0} if extra else {},
        compiler_params=pltpu.CompilerParams(vmem_limit_bytes=48 * 2**20, dimension_semantics=("arbitrary",)),
    )(*inputs, *extra)


def sum_body(count, *refs):
    total = refs[0][...]
    for ref in refs[1:count]:
        total = total + ref[...]
    refs[-1][0] = total


def sum_into(parts, layer, layers, held):
    block, width = parts[0].shape
    rows = block // 5
    spec = pl.BlockSpec((rows, width), lambda i: (i, 0))
    return into_layer(sum_body, parts, [spec] * len(parts), lambda layer: pl.BlockSpec((1, rows, width), lambda i: (layer, i, 0)), (5,), layer, (layers, block, width), held)


def sum_halves_body(count, *refs):
    half = refs[0].shape[2]
    for side in range(2):
        mine = refs[side:count:2]
        total = mine[0][0]
        for ref in mine[1:]:
            total = total + ref[0]
        refs[-1][0, :, side * half : (side + 1) * half] = total


def sum_halves_into(pairs, layer, layers, held):
    _, block, half = pairs[0][0].shape
    rows = block // 5
    flat = [part for pair in pairs for part in pair]
    spec = pl.BlockSpec((1, rows, half), lambda i: (0, i, 0))
    return into_layer(sum_halves_body, flat, [spec] * len(flat), lambda layer: pl.BlockSpec((1, rows, 2 * half), lambda i: (layer, i, 0)), (5,), layer, (layers, block, 2 * half), held)


def turn_body(layer0, *refs):
    out = refs[-1]
    block = refs[0].shape[-2]
    for side in range(2):
        total = refs[side][...]
        for ref in refs[2 + side : layer0 : 2]:
            total = total + ref[...]
        out[side, :, :block] = total.T
        total = refs[layer0 + side][0]
        for ref in refs[layer0 + 2 + side : -1 : 2]:
            total = total + ref[0]
        out[side, :, block:] = total.T


def turn(layer0, layer1):
    block, width = layer0[0].shape
    half, step = width // 2, 256
    blocks = half // step
    low = pl.BlockSpec((block, step), lambda j: (0, j))
    high = pl.BlockSpec((block, step), lambda j: (0, blocks + j))
    part = pl.BlockSpec((1, block, step), lambda j: (1, 0, j))
    flat0 = [array for array in layer0 for _ in range(2)]
    flat1 = [array for pair in layer1 for array in pair]
    out = pl.pallas_call(
        functools.partial(turn_body, len(flat0)),
        grid=(blocks,),
        out_shape=jax.ShapeDtypeStruct((2, half, 2 * block), jnp.float32),
        in_specs=[low, high] * len(layer0) + [part] * len(flat1),
        out_specs=pl.BlockSpec((2, step, 2 * block), lambda j: (0, j, 0)),
        compiler_params=pltpu.CompilerParams(vmem_limit_bytes=48 * 2**20, dimension_semantics=("arbitrary",)),
        name="turn",
    )(*flat0, *flat1)
    return out.reshape(DEVICES, width // DEVICES, 2 * block)


def join_body(blocks, out):
    block = blocks.shape[2] // 2
    for layer in range(2):
        for i in range(blocks.shape[0]):
            out[layer, :, i * block : (i + 1) * block] = blocks[i, :, layer * block : (layer + 1) * block]


def join(blocks):
    count, rows, both = blocks.shape
    step = 32
    return pl.pallas_call(
        join_body,
        grid=(rows // step,),
        out_shape=jax.ShapeDtypeStruct((2, rows, count * both // 2), jnp.float32),
        in_specs=[pl.BlockSpec((count, step, both), lambda i: (0, i, 0))],
        out_specs=pl.BlockSpec((2, step, count * both // 2), lambda i: (0, i, 0)),
        compiler_params=pltpu.CompilerParams(vmem_limit_bytes=48 * 2**20, dimension_semantics=("arbitrary",)),
        name="join",
    )(blocks)


def solution(mesh):
    def local_grads(tokens, targets, w_in, w_out):
        layers = w_in.shape[0]
        scale = (tokens.shape[0] * DEVICES) ** -0.5

        all_tokens, hidden1_all, grad1_all, grad0 = run_layers(tokens, targets, w_in, w_out, scale, 1)
        all_tokens, hidden1_all, grad1_all = (array.reshape(-1, tokens.shape[1]) for array in (all_tokens, hidden1_all, grad1_all))
        hidden1_all, grad1_all = [hidden1_all], [grad1_all]

        far_lo, far_hi, y_lo, y_hi, z_lo, z_hi, all_grad0 = column_grads(
            [(hidden1_all, grad1_all, 1, bits, True) for bits in (Y | Z, Y, Z)], w_in, w_out, grad0, 8, 0
        )
        all_grad0 = all_grad0.reshape(all_tokens.shape)
        far_lo = swap(far_lo, Y)
        far_hi = swap(far_hi, Z)
        y_lo = swap(y_lo, Y)
        z_hi = swap(z_hi, Z)
        second0_x, first0_x = column_grads([([all_tokens], [all_grad0], 0, X, False)], w_in, w_out)
        first0_x = swap(first0_x, X)
        second0_x = swap(second0_x, X)
        y_hi = swap(y_hi + far_hi, Y)
        z_lo = swap(z_lo + far_lo, Z)
        *own1, second0, first0 = column_grads([(hidden1_all, grad1_all, 1, 0, True), ([all_tokens], [all_grad0], 0, 0, False)], w_in, w_out)

        rows = turn([first0, first0_x], [own1, (y_lo, y_hi), (z_lo, z_hi)])
        rows = lax.all_to_all(rows, AXIS, split_axis=0, concat_axis=0, tiled=True)
        out_second = sum_halves_into([own1, (y_lo, y_hi), (z_lo, z_hi)], 1, layers, None)
        out_second = sum_into([second0, second0_x], 0, layers, out_second)
        out_first = join(rows)
        return out_first, out_second

    tok_spec = P(AXIS, None)
    grad_spec = P(None, AXIS, None)
    return jax.shard_map(local_grads, mesh=mesh, in_specs=(tok_spec, tok_spec, P(), P()), out_specs=(grad_spec, grad_spec), check_vma=False)
```

time: 1350 us -> 760 us (0.56)
  waiting for transfers between devices: 787 us -> 184 us
  Pallas kernels: 0 us -> 539 us
  matrix products: 452 us -> 0 us
  local copies, waits for them, and re-layouts: 80.5 us -> 3.75 us
    pallas_call x0 -> x8, Pallas kernels: none -> 539 us  [the longest x3 294 us: column_grads(): pl.pallas_call(functools.partial(grads_body, plan, len(arrays), len(out_s...]
    reduce_scatter x2 -> x0, waiting for transfers between devices: 523 us -> none  [local_grads(): lax.psum_scatter(grad_second, 'data', scatter_dimension=0, tiled=True)]
    dot_general x10 -> x0, matrix products: 416 us -> none  [the longest x2 110 us: local_grads(): jnp.einsum('td,fd->tf', grad_h, w_out[layer], preferred_element_type=jnp....]
    unnamed x6 -> x0, waiting for transfers between devices: 263 us -> none
    ppermute x0 -> x8, waiting for transfers between devices: none -> 184 us  [swap(): return lax.ppermute(value, AXIS, [(i, i ^ bits) for i in range(DEVICES)])]
    unnamed x16 -> x10, local copies, waits for them, and re-layouts: 80.5 us -> 3.75 us
    unnamed x1 -> x0, matrix products: 35.8 us -> none
  transfers between devices with their start and end apart: 4 -> 9, of which waited for: 3 -> 3; matrix products, arithmetic and copies ran while one was open for 22% -> 1% of each run, Pallas kernels for 0% -> 26%
where the time goes in v2:
time: 760 us; the launch traced here: 749 us
  Pallas kernels  539 us (71%)
  waiting for transfers between devices  184 us (24%)
  starting transfers between devices  12.3 us (2%)
  other arithmetic  9.46 us (1%)
    pallas_call x3, Pallas kernels, column_grads(): pl.pallas_call(functools.partial(grads_body, plan, len(arrays), len(out_s...  294 us
    pallas_call x1, Pallas kernels, run_layers(): pl.pallas_call(functools.partial(layers_body, scale, 2, tiles), grid=(3 *...  214 us
    ppermute x8, waiting for transfers between devices, swap(): return lax.ppermute(value, AXIS, [(i, i ^ bits) for i in range(DEVICES)])  184 us
  transfers between devices with their start and end apart: 9, of which 3 were waited for; matrix products, arithmetic and copies ran while one was open for 1% of the time, Pallas kernels for 26%

profile of v2, /device:TPU:0, one launch (start us, length us, event | category | flops | bytes accessed | tf_op | source)
XLA Modules:
  0.0 748.8 jit_solution(9734782883660412445)
XLA Ops:
  0.6 214.3 %run_layers.1 = (bf16[8,1024,1536]{2,1,0:T(8,128)(2,1)}, bf16[4,1024,1536]{2,1,0:T(8,128)(2,1)}, bf16[4,1024,1536]{2,1,0:T(8,128)(2,1)}, bf16[1024,1536]{1,0:T(8,128)(2,1)}) custom-call(bf16[1024,1536]{1,0:T(8,128)(2,1)} %refs_0_.1, bf16[1024,1536]{1,0:T(8,128)(2,1)} %refs_1_.1, bf16[2,1536,8960]{2,1,0:T(8,128)(2,1)} %refs_2_.3, bf16[2,8960,1536]{2,1,0:T(8,128)(2,1)} %refs_3_.5), custom_call_target="tpu_custom_call" | custom-call | flops 169114337280 | bytes 165150720 | tf_op jit(solution)/shard_map/run_layers/pallas_call | solution.py:414
  215.0 115.2 %column_grads.3 = (f32[2,560,768]{2,1,0:T(8,128)}, f32[2,560,768]{2,1,0:T(8,128)}, f32[2,560,768]{2,1,0:T(8,128)}, f32[2,560,768]{2,1,0:T(8,128)}, f32[2,560,768...) custom-call(bf16[4096,1536]{1,0:T(8,128)(2,1)} %bitcast.10, bf16[4096,1536]{1,0:T(8,128)(2,1)} %bitcast.12, ...), custom_call_target="tpu_custom_call" | custom-call | flops 84557168640 | bytes 106463232 | tf_op jit(solution)/shard_map/column_grads/pallas_call | solution.py:263
  330.2 1.6 collective-permute-start.4
  331.8 0.5 collective-permute-start.2
  332.3 1.5 collective-permute-start.1
  333.8 0.5 collective-permute-start.6
  334.3 72.7 %column_grads.5 = (f32[560,1536]{1,0:T(8,128)}, f32[560,1536]{1,0:T(8,128)}) custom-call(bf16[8192,1536]{1,0:T(8,128)(2,1)} %bitcast.6, bf16[8192,1536]{1,0:T(8,128)(2,1)} %bitcast.8, bf16[2,1536,8960]{2,1,0:T(8,128)(2,1)} %refs_2_.3, bf16[2,8960,1536]{2,1,0:T(8,128)(2,1)} %refs_3_.5), custom_call_target="tpu_custom_call" | custom-call | flops 56371445760 | bytes 60653568 | tf_op jit(solution)/shard_map/column_grads/pallas_call | solution.py:263
  407.0 0.6 collective-permute-start
  407.6 0.3 collective-permute-done.4
  407.9 5.3 add.7
  413.2 1.5 collective-permute-start.5
  414.7 4.2 add.6
  418.8 0.5 collective-permute-start.3
  419.3 106.6 %column_grads.4 = (f32[2,560,768]{2,1,0:T(8,128)}, f32[2,560,768]{2,1,0:T(8,128)}, f32[560,1536]{1,0:T(8,128)}, f32[560,1536]{1,0:T(8,128)}) custom-call(bf16[4096,1536]{1,0:T(8,128)(2,1)} %bitcast.11, bf16[4096,1536]{1,0:T(8,128)(2,1)} %bitcast.13, bf16[8192,1536]{1,0:T(8,128)(2,1)} %bitcast.7, bf16[8192,1536]{1,0:T(8,128)(2,1)} %bitcast.9, ...), custom_call_target="tpu_custom_call" | custom-call | flops 84557168640 | bytes 96141312 | tf_op jit(solution)/shard_map/column_grads/pallas_call | solution.py:263
  526.0 30.0 %collective-permute-done.5.refs_8_.refs_4_ = f32[2,560,768]{2,1,0:T(8,128)} collective-permute-done((f32[2,560,768]{2,1,0:T(8,128)}, f32[2,560,768]{2,1,0:T(8,128)}, u32[]{:S(2)}, u32[]{:S(2)}) %collective-permute-start.5) | collective-permute-done | bytes 3440672 | tf_op jit(solution)/shard_map/ppermute | solution.py:19
  556.0 2.0 copy-done
  557.9 10.1 %turn.1 = f32[2,768,1120]{2,1,0:T(8,128)} custom-call(f32[560,1536]{1,0:T(8,128)S(1)} %copy-done, f32[560,1536]{1,0:T(8,128)S(1)} %copy-done, f32[560,1536]{1,0:T(8,128)} %collective-permute-done.refs_2_.refs_3_, f32[560,1536]{1,0:T(8,128)} %collective-permute-done.refs_2_.refs_3_, f32[2,560,768]{2,1,0:T(8,128)} %get-tuple-element.26.refs_4_.refs_0_, ...), custom_call_target="tpu_custom_call" | custom-call | tf_op jit(solution)/shard_map/turn/pallas_call | solution.py:509
  568.0 3.8 all-to-all-start
  571.8 1.8 collective-permute-start.7
  573.6 6.6 shard_map.59.refs_2_
  580.2 153.2 %collective-permute-done.7.refs_1_ = f32[560,1536]{1,0:T(8,128)S(1)} collective-permute-done((f32[560,1536]{1,0:T(8,128)}, f32[560,1536]{1,0:T(8,128)S(1)}, u32[]{:S(2)}, u32[]{:S(2)}) %collective-permute-start.7) | collective-permute-done | bytes 3440672 | tf_op jit(solution)/shard_map/ppermute | solution.py:19
  733.4 1.8 copy-done.3
  735.1 5.5 shard_map.60
  740.6 7.7 %join.1 = f32[2,96,8960]{2,1,0:T(8,128)} custom-call(f32[16,96,1120]{2,1,0:T(8,128)} %all-to-all-done.blocks), custom_call_target="tpu_custom_call" | custom-call | tf_op jit(solution)/shard_map/join/pallas_call | solution.py:531
  (14 shorter events, 0.0 us)
Async XLA Ops:
  330.2 77.6 %collective-permute-start.4 = (f32[2,560,768]{2,1,0:T(8,128)}, f32[2,560,768]{2,1,0:T(8,128)}, u32[]{:S(2)}, u32[]{:S(2)}) collective-permute-start(f32[2,560,768]{2,1,0:T(8,128)} %get-tuple-element.32), channel_id=1, source_target_pairs={{0,4},{1,5},{2,6},{3,7},{4,0},{5,1},{6,2},{7,3},{8,12},{9,13},{10,... | collective-permute-start | bytes 10321928 | tf_op jit(solution)/shard_map/ppermute | solution.py:19
  331.8 82.9 %collective-permute-start.2 = (f32[2,560,768]{2,1,0:T(8,128)}, f32[2,560,768]{2,1,0:T(8,128)}, u32[]{:S(2)}, u32[]{:S(2)}) collective-permute-start(f32[2,560,768]{2,1,0:T(8,128)} %get-tuple-element.30), channel_id=1, source_target_pairs={{0,8},{1,9},{2,10},{3,11},{4,12},{5,13},{6,14},{7,15},{8,0},{9,1},... | collective-permute-start | bytes 10321928 | tf_op jit(solution)/shard_map/ppermute | solution.py:19
  332.3 193.7 %collective-permute-start.1 = (f32[2,560,768]{2,1,0:T(8,128)}, f32[2,560,768]{2,1,0:T(8,128)}, u32[]{:S(2)}, u32[]{:S(2)}) collective-permute-start(f32[2,560,768]{2,1,0:T(8,128)} %get-tuple-element.28), channel_id=1, source_target_pairs={{0,4},{1,5},{2,6},{3,7},{4,0},{5,1},{6,2},{7,3},{8,12},{9,13},{10,... | collective-permute-start | bytes 10321928 | tf_op jit(solution)/shard_map/ppermute | solution.py:19
  333.8 192.1 %collective-permute-start.6 = (f32[2,560,768]{2,1,0:T(8,128)}, f32[2,560,768]{2,1,0:T(8,128)}, u32[]{:S(2)}, u32[]{:S(2)}) collective-permute-start(f32[2,560,768]{2,1,0:T(8,128)} %get-tuple-element.33), channel_id=1, source_target_pairs={{0,8},{1,9},{2,10},{3,11},{4,12},{5,13},{6,14},{7,15},{8,0},{9,1},... | collective-permute-start | bytes 10321928 | tf_op jit(solution)/shard_map/ppermute | solution.py:19
  407.0 119.0 %collective-permute-start = (f32[560,1536]{1,0:T(8,128)}, f32[560,1536]{1,0:T(8,128)}, u32[]{:S(2)}, u32[]{:S(2)}) collective-permute-start(f32[560,1536]{1,0:T(8,128)} %get-tuple-element.25), channel_id=1, source_target_pairs={{0,2},{1,3},{2,0},{3,1},{4,6},{5,7},{6,4},{7,5},{8,10},{9,11},{10,... | collective-permute-start | bytes 10321928 | tf_op jit(solution)/shard_map/ppermute | solution.py:19
  407.8 6.8 copy-start.4
  413.2 142.8 %collective-permute-start.5 = (f32[2,560,768]{2,1,0:T(8,128)}, f32[2,560,768]{2,1,0:T(8,128)}, u32[]{:S(2)}, u32[]{:S(2)}) collective-permute-start(f32[2,560,768]{2,1,0:T(8,128)} %add.7), channel_id=1, source_target_pairs={{0,8},{1,9},{2,10},{3,11},{4,12},{5,13},{6,14},{7,15},{8,0},{9,1},... | collective-permute-start | bytes 10321928 | tf_op jit(solution)/shard_map/ppermute | solution.py:19
  418.8 137.1 %collective-permute-start.3 = (f32[2,560,768]{2,1,0:T(8,128)}, f32[2,560,768]{2,1,0:T(8,128)}, u32[]{:S(2)}, u32[]{:S(2)}) collective-permute-start(f32[2,560,768]{2,1,0:T(8,128)} %add.6), channel_id=1, source_target_pairs={{0,4},{1,5},{2,6},{3,7},{4,0},{5,1},{6,2},{7,3},{8,12},{9,13},{10,... | collective-permute-start | bytes 10321928 | tf_op jit(solution)/shard_map/ppermute | solution.py:19
  556.0 2.0 copy-start
  568.0 5.6 copy-start.1
  568.0 172.6 %all-to-all-start = ((f32[16,96,1120]{2,1,0:T(8,128)}), f32[16,96,1120]{2,1,0:T(8,128)}, u32[]{:S(2)}, u32[]{:S(2)}) async-start(f32[16,96,1120]{2,1,0:T(8,128)} %bitcast.5), calls=%async_computation | async-start | bytes 14155776 | tf_op jit(solution)/shard_map/all_to_all | solution.py:567
  571.8 163.3 %copy-start.2 = (f32[560,1536]{1,0:T(8,128)S(1)}, f32[560,1536]{1,0:T(8,128)}, u32[]{:S(2)}) copy-start(f32[560,1536]{1,0:T(8,128)} %get-tuple-element.34.refs_0_) | copy-start | bytes 10321924
  571.8 161.5 %collective-permute-start.7 = (f32[560,1536]{1,0:T(8,128)}, f32[560,1536]{1,0:T(8,128)S(1)}, u32[]{:S(2)}, u32[]{:S(2)}) collective-permute-start(f32[560,1536]{1,0:T(8,128)} %get-tuple-element.35), channel_id=1, source_target_pairs={{0,2},{1,3},{2,0},{3,1},{4,6},{5,7},{6,4},{7,5},{8,10},{9,11},{10,... | collective-permute-start | bytes 10321928 | tf_op jit(solution)/shard_map/ppermute | solution.py:19
  733.4 1.8 copy-start.3

commit v3 on v2

--- a/solution.py
+++ b/solution.py
@@ -44,6 +44,10 @@
         if bits & bit:
             index = index + bit - 2 * bit * (index // bit % 2)
     return index
+
+
+def pair_rank(index):
+    return index // X % 2 * 2 + index % 2
 
 
 def plane_rank(index):
@@ -87,12 +91,14 @@
 GATHER_SEMS = [pltpu.SemaphoreType.DMA((9,)), pltpu.SemaphoreType.DMA((9,)), pltpu.SemaphoreType.DMA((1,))]
 
 
-def grads_body(plan, count, outs, tile, parts, turn_at, *refs):
-    arrays = refs[:count]
+def grads_body(plan, count, outs, tile, parts, turn_at, late, *refs):
+    arrays = list(refs[:count])
     w_in, w_out = refs[count : count + 2]
     own_block = arrays[-1]
     outputs = refs[count + 2 : count + 2 + outs]
     hidden_buf, grad_buf, act_buf, pre_buf, window, w_in_t, w_out_buf, acc, sem, w_sem, out_sem = refs[count + 2 + outs : count + 13 + outs]
+    if late is not None:
+        arrays[late] = outputs[-1]
     gather_sems = refs[count + 13 + outs :]
     block, width = w_in_t.shape
     span = window.shape[1]
@@ -104,7 +110,7 @@
         begins.append(at)
         for h, g in zip(segment["hidden"], segment["grad"]):
             tiles = arrays[h].shape[0] // tile
-            sources.append((at, at + tiles, arrays[h], arrays[g]))
+            sources.append((at, at + tiles, arrays[h], arrays[g], segment["layer"]))
             at += tiles
     ends = begins[1:] + [at]
     index = sum([(step >= begin).astype(jnp.int32) for begin in begins[1:]], jnp.int32(0))
@@ -114,10 +120,13 @@
         fresh = fresh | (step == begin)
 
     def fetch(at, slot):
-        for begin, end, hidden, grad in sources:
+        for begin, end, hidden, grad, layer in sources:
             @pl.when((at >= begin) & (at < end))
             def _():
-                rows = pl.ds(pl.multiple_of((at - begin) * tile, tile), tile)
+                place = at - begin
+                if layer == 1:
+                    place = (me // X + place // 2) % 2 * 2 + (me + place) % 2
+                rows = pl.ds(pl.multiple_of(place * tile, tile), tile)
                 pltpu.make_async_copy(hidden.at[rows], hidden_buf.at[slot], sem.at[0, slot]).start()
                 pltpu.make_async_copy(grad.at[rows], grad_buf.at[slot], sem.at[1, slot]).start()
 
@@ -149,13 +158,21 @@
         fetch(0, 0)
 
     if turn_at is not None:
-        barrier, keep, first, second, last = plane_gather(own_block, outputs[-1], *gather_sems)
+        barrier, keep, first, second, last = plane_gather(own_block, outputs[-2], *gather_sems[:3])
+        far = arrays[late].at[pl.ds(pl.multiple_of(pair_rank(flipped(me, X)) * tile, tile), tile)]
+        far_copy = pltpu.make_async_remote_copy(
+            src_ref=far, dst_ref=far, send_sem=gather_sems[3].at[0], recv_sem=gather_sems[3].at[1], device_id=(flipped(me, CORE),), device_id_type=pl.DeviceIdType.MESH
+        )
 
         @pl.when(step == 0)
         def _():
             barrier()
-            for copy in first + [keep]:
+            for copy in first + [keep, far_copy]:
                 copy.start()
+
+        @pl.when(step == 2)
+        def _():
+            far_copy.wait_recv()
 
         @pl.when(step == turn_at)
         def _():
@@ -164,18 +181,23 @@
             for copy in second:
                 copy.start()
 
-    for k, begin in enumerate(begins):
-        @pl.when(step == begin)
+    @pl.when(fresh)
+    def _():
+        copies = weights(0)[1]
+        copies[0].wait()
+        shift = weights(0)[0]
+        for k in range(1, len(plan)):
+            shift = jnp.where(index == k, weights(k)[0], shift)
+        chosen = lax.broadcasted_iota(jnp.int32, (block, span), 0) + shift
+        chosen = (chosen == lax.broadcasted_iota(jnp.int32, (block, span), 1)).astype(jnp.bfloat16)
+        w_in_t[...] = dot_nt(chosen, window[...]).astype(jnp.bfloat16)
+        copies[1].wait()
+
+    for k in range(2, len(plan)):
+        @pl.when(step == begins[k])
         def _(k=k):
-            shift, copies = weights(k)
-            copies[0].wait()
-            chosen = lax.broadcasted_iota(jnp.int32, (block, span), 0) + shift
-            chosen = (chosen == lax.broadcasted_iota(jnp.int32, (block, span), 1)).astype(jnp.bfloat16)
-            w_in_t[...] = dot_nt(chosen, window[...]).astype(jnp.bfloat16)
-            copies[1].wait()
-            if k >= 2:
-                for copy in results(k - 2, 0) + results(k - 2, 1):
-                    copy.wait()
+            for copy in results(k - 2, 0) + results(k - 2, 1):
+                copy.wait()
 
     for k, end in enumerate(ends[:-1]):
         @pl.when(step == end - 1)
@@ -227,14 +249,14 @@
             first[2].wait_recv()
             for copy in second[2:] + last:
                 copy.wait_recv()
-            for copy in first + second + last:
+            for copy in first + second + last + [far_copy]:
                 copy.wait_send()
         for k in range(max(0, len(plan) - 2), len(plan)):
             for copy in results(k, 0) + results(k, 1):
                 copy.wait()
 
 
-def column_grads(segments, w_in, w_out, gathered=None, turn_at=None, collective_id=None):
+def column_grads(segments, w_in, w_out, gathered=None, turn_at=None, unfinished=None, collective_id=None):
     arrays, plan = [], []
 
     def place(array):
@@ -254,14 +276,17 @@
     shapes = [(2, block, width // 2) if segment["split"] else (block, width) for segment in plan for _ in range(2)]
     out_shape = [jax.ShapeDtypeStruct(shape, jnp.float32) for shape in shapes]
     bf16 = jnp.bfloat16
-    params = {}
+    params, late, aliases = {}, None, {}
     if gathered is not None:
+        late = place(unfinished)
         arrays.append(gathered)
         out_shape.append(jax.ShapeDtypeStruct((8,) + gathered.shape, bf16))
+        out_shape.append(jax.ShapeDtypeStruct(unfinished.shape, bf16))
+        aliases = {late: len(out_shape) - 1}
         params = dict(collective_id=collective_id, has_side_effects=True)
     hbm = pl.BlockSpec(memory_space=pl.ANY)
     return pl.pallas_call(
-        functools.partial(grads_body, plan, len(arrays), len(out_shape), tile, 2, turn_at),
+        functools.partial(grads_body, plan, len(arrays), len(out_shape), tile, 2, turn_at, late),
         grid=(tokens // tile,),
         out_shape=out_shape,
         in_specs=[hbm] * (len(arrays) + 2),
@@ -271,7 +296,8 @@
         + [pltpu.VMEM((width, span), bf16), pltpu.VMEM((block, width), bf16), pltpu.VMEM((2, block, width), bf16)]
         + [pltpu.VMEM((2, 2, block, width), jnp.float32)]
         + [pltpu.SemaphoreType.DMA((2, 2)), pltpu.SemaphoreType.DMA((2,)), pltpu.SemaphoreType.DMA((2, 4))]
-        + (GATHER_SEMS if gathered is not None else []),
+        + (GATHER_SEMS + [pltpu.SemaphoreType.DMA((2,))] if gathered is not None else []),
+        input_output_aliases=aliases,
         compiler_params=pltpu.CompilerParams(vmem_limit_bytes=62 * 2**20, dimension_semantics=("arbitrary",), **params),
         cost_estimate=pl.CostEstimate(
             flops=8 * tokens * block * width, bytes_accessed=4 * tokens * width + 12 * block * width * len(plan), transcendentals=tokens * block
@@ -281,10 +307,6 @@
 
 
 FF_TILE = 1280
-
-
-def pair_rank(index):
-    return index // X % 2 * 2 + index % 2
 
 
 def layers_body(scale, parts, tiles, *refs):
@@ -304,9 +326,9 @@
 
     def pair(array, n):
         store = pltpu.make_async_copy(now, array.at[pair_rank(me)], local.at[n])
-        return store, remote(array, 0, X, 3 * n), remote(array, 0, CORE, 3 * n + 1), remote(array, X, CORE, 3 * n + 2)
-
-    hidden_copies, grad_copies = pair(hidden_all, 0), pair(grad_all, 1)
+        return store, remote(array, 0, X, 3 * n), remote(array, 0, CORE, 3 * n + 1)
+
+    hidden_copies, grad_copies = pair(hidden_all, 0) + (remote(hidden_all, X, CORE, 2),), pair(grad_all, 1)
     get_tokens = pltpu.make_async_copy(tokens, now, local.at[2])
     get_target = pltpu.make_async_copy(targets, target, local.at[3])
     put_below = pltpu.make_async_copy(now, below, local.at[4])
@@ -391,17 +413,15 @@
         now[...] = acc[...].astype(jnp.bfloat16)
         put_below.start()
         grad_copies[1].wait_recv()
-        grad_copies[3].start()
         keep.wait()
         put_below.wait()
         first[2].wait_recv()
         for copy in second[2:] + last:
             copy.wait_recv()
-        for copies in (hidden_copies, grad_copies):
-            copies[2].wait_recv()
-            copies[3].wait_recv()
-            for copy in copies[1:]:
-                copy.wait_send()
+        for copy in hidden_copies[2:] + grad_copies[2:3]:
+            copy.wait_recv()
+        for copy in hidden_copies[1:] + grad_copies[1:3]:
+            copy.wait_send()
         for copy in first + second + last:
             copy.wait_send()
 
@@ -447,7 +467,7 @@
         in_specs=in_specs + [pl.BlockSpec(memory_space=pl.ANY)] * len(extra),
         out_specs=spec_of(layer),
         input_output_aliases={len(inputs): 0} if extra else {},
-        compiler_params=pltpu.CompilerParams(vmem_limit_bytes=48 * 2**20, dimension_semantics=("arbitrary",)),
+        compiler_params=pltpu.CompilerParams(vmem_limit_bytes=62 * 2**20, dimension_semantics=("arbitrary",)),
     )(*inputs, *extra)
 
 
@@ -483,60 +503,51 @@
     return into_layer(sum_halves_body, flat, [spec] * len(flat), lambda layer: pl.BlockSpec((1, rows, 2 * half), lambda i: (layer, i, 0)), (5,), layer, (layers, block, 2 * half), held)
 
 
-def turn_body(layer0, *refs):
+def turn_body(lead, *refs):
+    for side in range(2):
+        total = refs[side][lead]
+        for ref in refs[2 + side : -1 : 2]:
+            total = total + ref[lead]
+        refs[-1][side] = total.T
+
+
+def turn(parts):
+    pairs = isinstance(parts[0], (list, tuple))
+    block, half = (parts[0][0].shape if pairs else parts[0].shape)[-2:]
+    half = half if pairs else half // 2
+    step = 256
+    blocks = half // step
+    if pairs:
+        specs = [pl.BlockSpec((1, block, step), lambda j: (1, 0, j))] * 2
+        flat = [array for pair in parts for array in pair]
+    else:
+        specs = [pl.BlockSpec((block, step), lambda j: (0, j)), pl.BlockSpec((block, step), lambda j: (0, blocks + j))]
+        flat = [array for array in parts for _ in range(2)]
+    out = pl.pallas_call(
+        functools.partial(turn_body, 0 if pairs else slice(None)),
+        grid=(blocks,),
+        out_shape=jax.ShapeDtypeStruct((2, half, block), jnp.float32),
+        in_specs=specs * len(parts),
+        out_specs=pl.BlockSpec((2, step, block), lambda j: (0, j, 0)),
+        compiler_params=pltpu.CompilerParams(vmem_limit_bytes=62 * 2**20, dimension_semantics=("arbitrary",)),
+    )(*flat)
+    return out.reshape(DEVICES, 2 * half // DEVICES, block)
+
+
+def join_body(count, blocks, *refs):
     out = refs[-1]
-    block = refs[0].shape[-2]
-    for side in range(2):
-        total = refs[side][...]
-        for ref in refs[2 + side : layer0 : 2]:
-            total = total + ref[...]
-        out[side, :, :block] = total.T
-        total = refs[layer0 + side][0]
-        for ref in refs[layer0 + 2 + side : -1 : 2]:
-            total = total + ref[0]
-        out[side, :, block:] = total.T
-
-
-def turn(layer0, layer1):
-    block, width = layer0[0].shape
-    half, step = width // 2, 256
-    blocks = half // step
-    low = pl.BlockSpec((block, step), lambda j: (0, j))
-    high = pl.BlockSpec((block, step), lambda j: (0, blocks + j))
-    part = pl.BlockSpec((1, block, step), lambda j: (1, 0, j))
-    flat0 = [array for array in layer0 for _ in range(2)]
-    flat1 = [array for pair in layer1 for array in pair]
-    out = pl.pallas_call(
-        functools.partial(turn_body, len(flat0)),
-        grid=(blocks,),
-        out_shape=jax.ShapeDtypeStruct((2, half, 2 * block), jnp.float32),
-        in_specs=[low, high] * len(layer0) + [part] * len(flat1),
-        out_specs=pl.BlockSpec((2, step, 2 * block), lambda j: (0, j, 0)),
-        compiler_params=pltpu.CompilerParams(vmem_limit_bytes=48 * 2**20, dimension_semantics=("arbitrary",)),
-        name="turn",
-    )(*flat0, *flat1)
-    return out.reshape(DEVICES, width // DEVICES, 2 * block)
-
-
-def join_body(blocks, out):
-    block = blocks.shape[2] // 2
-    for layer in range(2):
-        for i in range(blocks.shape[0]):
-            out[layer, :, i * block : (i + 1) * block] = blocks[i, :, layer * block : (layer + 1) * block]
-
-
-def join(blocks):
-    count, rows, both = blocks.shape
+    block = blocks.shape[2]
+    for i in range(blocks.shape[0]):
+        out[0, :, i * block : (i + 1) * block] = blocks[i]
+
+
+def join_into(blocks, layer, layers, held):
+    count, rows, block = blocks.shape
     step = 32
-    return pl.pallas_call(
-        join_body,
-        grid=(rows // step,),
-        out_shape=jax.ShapeDtypeStruct((2, rows, count * both // 2), jnp.float32),
-        in_specs=[pl.BlockSpec((count, step, both), lambda i: (0, i, 0))],
-        out_specs=pl.BlockSpec((2, step, count * both // 2), lambda i: (0, i, 0)),
-        compiler_params=pltpu.CompilerParams(vmem_limit_bytes=48 * 2**20, dimension_semantics=("arbitrary",)),
-        name="join",
-    )(blocks)
+    in_spec = pl.BlockSpec((count, step, block), lambda i: (0, i, 0))
+    return into_layer(
+        join_body, [blocks], [in_spec], lambda layer: pl.BlockSpec((1, step, count * block), lambda i: (layer, i, 0)), (rows // step,), layer, (layers, rows, count * block), held
+    )
 
 
 def solution(mesh):
@@ -546,11 +557,12 @@
 
         all_tokens, hidden1_all, grad1_all, grad0 = run_layers(tokens, targets, w_in, w_out, scale, 1)
         all_tokens, hidden1_all, grad1_all = (array.reshape(-1, tokens.shape[1]) for array in (all_tokens, hidden1_all, grad1_all))
-        hidden1_all, grad1_all = [hidden1_all], [grad1_all]
-
-        far_lo, far_hi, y_lo, y_hi, z_lo, z_hi, all_grad0 = column_grads(
-            [(hidden1_all, grad1_all, 1, bits, True) for bits in (Y | Z, Y, Z)], w_in, w_out, grad0, 8, 0
+        hidden1_all = [hidden1_all]
+
+        far_lo, far_hi, y_lo, y_hi, z_lo, z_hi, all_grad0, grad1_all = column_grads(
+            [(hidden1_all, [grad1_all], 1, bits, True) for bits in (Y | Z, Y, Z)], w_in, w_out, grad0, 8, grad1_all, 0
         )
+        grad1_all = [grad1_all]
         all_grad0 = all_grad0.reshape(all_tokens.shape)
         far_lo = swap(far_lo, Y)
         far_hi = swap(far_hi, Z)
@@ -563,11 +575,17 @@
         z_lo = swap(z_lo + far_lo, Z)
         *own1, second0, first0 = column_grads([(hidden1_all, grad1_all, 1, 0, True), ([all_tokens], [all_grad0], 0, 0, False)], w_in, w_out)
 
-        rows = turn([first0, first0_x], [own1, (y_lo, y_hi), (z_lo, z_hi)])
-        rows = lax.all_to_all(rows, AXIS, split_axis=0, concat_axis=0, tiled=True)
+        def exchange(first):
+            return lax.all_to_all(first, AXIS, split_axis=0, concat_axis=0, tiled=True)
+
+        first0 = turn([first0, first0_x])
+        first0 = exchange(first0)
+        first1 = turn([own1, (y_lo, y_hi), (z_lo, z_hi)])
+        first1 = exchange(first1)
         out_second = sum_halves_into([own1, (y_lo, y_hi), (z_lo, z_hi)], 1, layers, None)
         out_second = sum_into([second0, second0_x], 0, layers, out_second)
-        out_first = join(rows)
+        out_first = join_into(first0, 0, layers, None)
+        out_first = join_into(first1, 1, layers, out_first)
         return out_first, out_second
 
     tok_spec = P(AXIS, None)

time: 760 us -> 710 us (0.934)
  waiting for transfers between devices: 184 us -> 132 us
    ppermute x8, waiting for transfers between devices: 184 us -> 90.5 us  [swap(): return lax.ppermute(value, AXIS, [(i, i ^ bits) for i in range(DEVICES)])]
    all_to_all x1 -> x2, waiting for transfers between devices: 0.01 us -> 41.9 us  [exchange(): return lax.all_to_all(first, AXIS, split_axis=0, concat_axis=0, tiled=True)]
    pallas_call x2 -> x4, Pallas kernels: 12 us -> 23.5 us  [into_layer(): pl.pallas_call(functools.partial(body, len(inputs)), grid=grid, out_shape...]
  transfers between devices with their start and end apart: 9 -> 10, of which waited for: 3 -> 5; matrix products, arithmetic and copies ran while one was open for 1% -> 1% of each run, Pallas kernels for 26% -> 30%
where the time goes in v3:
time: 710 us; the launch traced here: 699 us
  Pallas kernels  540 us (76%)
  waiting for transfers between devices  132 us (19%)
  starting transfers between devices  16 us (2%)
  other arithmetic  9.49 us (1%)
    pallas_call x3, Pallas kernels, column_grads(): pl.pallas_call(functools.partial(grads_body, plan, len(arrays), len(out_s...  294 us
    pallas_call x1, Pallas kernels, run_layers(): pl.pallas_call(functools.partial(layers_body, scale, 2, tiles), grid=(3 *...  209 us
    ppermute x8, waiting for transfers between devices, swap(): return lax.ppermute(value, AXIS, [(i, i ^ bits) for i in range(DEVICES)])  90.5 us
    all_to_all x2, waiting for transfers between devices, exchange(): return lax.all_to_all(first, AXIS, split_axis=0, concat_axis=0, tiled=True)  41.9 us
    pallas_call x4, Pallas kernels, into_layer(): pl.pallas_call(functools.partial(body, len(inputs)), grid=grid, out_shape...  23.5 us
  transfers between devices with their start and end apart: 10, of which 5 were waited for; matrix products, arithmetic and copies ran while one was open for 1% of the time, Pallas kernels for 30%

profile of v3, /device:TPU:0, one launch (start us, length us, event | category | flops | bytes accessed | tf_op | source)
XLA Modules:
  0.0 698.5 jit_solution(10331981328342956171)
XLA Ops:
  0.6 209.0 %run_layers.1 = (bf16[8,1024,1536]{2,1,0:T(8,128)(2,1)}, bf16[4,1024,1536]{2,1,0:T(8,128)(2,1)}, bf16[4,1024,1536]{2,1,0:T(8,128)(2,1)}, bf16[1024,1536]{1,0:T(8,128)(2,1)}) custom-call(bf16[1024,1536]{1,0:T(8,128)(2,1)} %refs_0_.1, bf16[1024,1536]{1,0:T(8,128)(2,1)} %refs_1_.1, bf16[2,1536,8960]{2,1,0:T(8,128)(2,1)} %refs_2_.3, bf16[2,8960,1536]{2,1,0:T(8,128)(2,1)} %refs_3_.5), custom_call_target="tpu_custom_call" | custom-call | flops 169114337280 | bytes 165150720 | tf_op jit(solution)/shard_map/run_layers/pallas_call | solution.py:434
  209.7 114.5 %column_grads.3 = (f32[2,560,768]{2,1,0:T(8,128)}, f32[2,560,768]{2,1,0:T(8,128)}, f32[2,560,768]{2,1,0:T(8,128)}, f32[2,560,768]{2,1,0:T(8,128)}, f32[2,560,768...) custom-call(bf16[4096,1536]{1,0:T(8,128)(2,1)} %bitcast.12, ...), custom_call_target="tpu_custom_call", output_to_operand_aliasing={{7}: (1, {})} | custom-call | flops 84557168640 | bytes 106463232 | tf_op jit(solution)/shard_map/column_grads/pallas_call | solution.py:288
  324.2 1.6 collective-permute-start.1
  325.7 0.9 collective-permute-start.3
  326.6 72.7 %column_grads.5 = (f32[560,1536]{1,0:T(8,128)}, f32[560,1536]{1,0:T(8,128)}) custom-call(bf16[8192,1536]{1,0:T(8,128)(2,1)} %bitcast.8, bf16[8192,1536]{1,0:T(8,128)(2,1)} %bitcast.10, bf16[2,1536,8960]{2,1,0:T(8,128)(2,1)} %refs_2_.3, bf16[2,8960,1536]{2,1,0:T(8,128)(2,1)} %refs_3_.5), custom_call_target="tpu_custom_call" | custom-call | flops 56371445760 | bytes 60653568 | tf_op jit(solution)/shard_map/column_grads/pallas_call | solution.py:288
  399.9 1.2 collective-permute-start
  401.6 5.3 add.6
  407.0 1.5 collective-permute-start.2
  408.5 4.2 add.7
  413.5 107.1 %column_grads.4 = (f32[2,560,768]{2,1,0:T(8,128)}, f32[2,560,768]{2,1,0:T(8,128)}, f32[560,1536]{1,0:T(8,128)}, f32[560,1536]{1,0:T(8,128)}) custom-call(bf16[4096,1536]{1,0:T(8,128)(2,1)} %bitcast.13, bf16[4096,1536]{1,0:T(8,128)(2,1)} %get-tuple-element.23.refs_1_, bf16[8192,1536]{1,0:T(8,128)(2,1)} %bitcast.9, bf16[8192,1536]{1,0:T(8,128)(2,1)} %bitcast.11, ...), custom_call_target="tpu_custom_call" | custom-call | flops 84557168640 | bytes 96141312 | tf_op jit(solution)/shard_map/column_grads/pallas_call | solution.py:288
  520.5 6.1 shard_map.60
  526.6 3.3 all-to-all-start.1
  529.9 1.7 collective-permute-start.7
  531.7 35.4 %collective-permute-done.2.refs_3_ = f32[2,560,768]{2,1,0:T(8,128)} collective-permute-done((f32[2,560,768]{2,1,0:T(8,128)}, f32[2,560,768]{2,1,0:T(8,128)}, u32[]{:S(2)}, u32[]{:S(2)}) %collective-permute-start.2) | collective-permute-done | bytes 3440672 | tf_op jit(solution)/shard_map/ppermute | solution.py:19
  567.0 11.7 %collective-permute-done.4.refs_4_ = f32[2,560,768]{2,1,0:T(8,128)} collective-permute-done((f32[2,560,768]{2,1,0:T(8,128)}, f32[2,560,768]{2,1,0:T(8,128)}, u32[]{:S(2)}, u32[]{:S(2)}) %collective-permute-start.4) | collective-permute-done | bytes 3440672 | tf_op jit(solution)/shard_map/ppermute | solution.py:19
  578.8 6.9 shard_map.59
  585.7 5.5 all-to-all-done.1.blocks
  591.2 3.9 all-to-all-start
  595.0 5.2 shard_map.61.refs_0_
  600.3 6.9 shard_map.63.refs_2_
  607.2 43.3 %collective-permute-done.7.refs_1_ = f32[560,1536]{1,0:T(8,128)} collective-permute-done((f32[560,1536]{1,0:T(8,128)}, f32[560,1536]{1,0:T(8,128)}, u32[]{:S(2)}, u32[]{:S(2)}) %collective-permute-start.7) | collective-permute-done | bytes 3440672 | tf_op jit(solution)/shard_map/ppermute | solution.py:19
  650.5 6.2 shard_map.64
  656.7 36.4 %all-to-all-done.blocks = f32[16,96,560]{2,1,0:T(8,128)} async-done(((f32[16,96,560]{2,1,0:T(8,128)}), f32[16,96,560]{2,1,0:T(8,128)}, u32[]{:S(2)}, u32[]{:S(2)}) %all-to-all-start) | async-done | bytes 3440672 | tf_op jit(solution)/shard_map/all_to_all | solution.py:579
  693.1 5.2 shard_map.62
  (10 shorter events, 2.0 us)
Async XLA Ops:
  324.2 77.5 %collective-permute-start.1 = (f32[2,560,768]{2,1,0:T(8,128)}, f32[2,560,768]{2,1,0:T(8,128)}, u32[]{:S(2)}, u32[]{:S(2)}) collective-permute-start(f32[2,560,768]{2,1,0:T(8,128)} %get-tuple-element.30), channel_id=1, source_target_pairs={{0,8},{1,9},{2,10},{3,11},{4,12},{5,13},{6,14},{7,15},{8,0},{9,1},... | collective-permute-start | bytes 10321928 | tf_op jit(solution)/shard_map/ppermute | solution.py:19
  325.7 82.7 %collective-permute-start.3 = (f32[2,560,768]{2,1,0:T(8,128)}, f32[2,560,768]{2,1,0:T(8,128)}, u32[]{:S(2)}, u32[]{:S(2)}) collective-permute-start(f32[2,560,768]{2,1,0:T(8,128)} %get-tuple-element.32), channel_id=1, source_target_pairs={{0,4},{1,5},{2,6},{3,7},{4,0},{5,1},{6,2},{7,3},{8,12},{9,13},{10,... | collective-permute-start | bytes 10321928 | tf_op jit(solution)/shard_map/ppermute | solution.py:19
  399.3 121.2 %collective-permute-start.6 = (f32[560,1536]{1,0:T(8,128)}, f32[560,1536]{1,0:T(8,128)}, u32[]{:S(2)}, u32[]{:S(2)}) collective-permute-start(f32[560,1536]{1,0:T(8,128)} %get-tuple-element.35), channel_id=1, source_target_pairs={{0,2},{1,3},{2,0},{3,1},{4,6},{5,7},{6,4},{7,5},{8,10},{9,11},{10,... | collective-permute-start | bytes 10321928 | tf_op jit(solution)/shard_map/ppermute | solution.py:19
  399.9 131.8 %collective-permute-start = (f32[2,560,768]{2,1,0:T(8,128)}, f32[2,560,768]{2,1,0:T(8,128)}, u32[]{:S(2)}, u32[]{:S(2)}) collective-permute-start(f32[2,560,768]{2,1,0:T(8,128)} %get-tuple-element.28), channel_id=1, source_target_pairs={{0,4},{1,5},{2,6},{3,7},{4,0},{5,1},{6,2},{7,3},{8,12},{9,13},{10,... | collective-permute-start | bytes 10321928 | tf_op jit(solution)/shard_map/ppermute | solution.py:19
  401.1 130.6 %collective-permute-start.5 = (f32[2,560,768]{2,1,0:T(8,128)}, f32[2,560,768]{2,1,0:T(8,128)}, u32[]{:S(2)}, u32[]{:S(2)}) collective-permute-start(f32[2,560,768]{2,1,0:T(8,128)} %get-tuple-element.33), channel_id=1, source_target_pairs={{0,8},{1,9},{2,10},{3,11},{4,12},{5,13},{6,14},{7,15},{8,0},{9,1},... | collective-permute-start | bytes 10321928 | tf_op jit(solution)/shard_map/ppermute | solution.py:19
  401.6 6.8 copy-start
  407.0 160.1 %collective-permute-start.2 = (f32[2,560,768]{2,1,0:T(8,128)}, f32[2,560,768]{2,1,0:T(8,128)}, u32[]{:S(2)}, u32[]{:S(2)}) collective-permute-start(f32[2,560,768]{2,1,0:T(8,128)} %add.6), channel_id=1, source_target_pairs={{0,4},{1,5},{2,6},{3,7},{4,0},{5,1},{6,2},{7,3},{8,12},{9,13},{10,... | collective-permute-start | bytes 10321928 | tf_op jit(solution)/shard_map/ppermute | solution.py:19
  412.6 166.1 %collective-permute-start.4 = (f32[2,560,768]{2,1,0:T(8,128)}, f32[2,560,768]{2,1,0:T(8,128)}, u32[]{:S(2)}, u32[]{:S(2)}) collective-permute-start(f32[2,560,768]{2,1,0:T(8,128)} %add.7), channel_id=1, source_target_pairs={{0,8},{1,9},{2,10},{3,11},{4,12},{5,13},{6,14},{7,15},{8,0},{9,1},... | collective-permute-start | bytes 10321928 | tf_op jit(solution)/shard_map/ppermute | solution.py:19
  526.6 64.6 %all-to-all-start.1 = ((f32[16,96,560]{2,1,0:T(8,128)}), f32[16,96,560]{2,1,0:T(8,128)}, u32[]{:S(2)}, u32[]{:S(2)}) async-start(f32[16,96,560]{2,1,0:T(8,128)} %bitcast.6), calls=%async_computation.1 | async-start | bytes 7864320 | tf_op jit(solution)/shard_map/all_to_all | solution.py:579
  529.9 120.6 %collective-permute-start.7 = (f32[560,1536]{1,0:T(8,128)}, f32[560,1536]{1,0:T(8,128)}, u32[]{:S(2)}, u32[]{:S(2)}) collective-permute-start(f32[560,1536]{1,0:T(8,128)} %get-tuple-element.37), channel_id=1, source_target_pairs={{0,2},{1,3},{2,0},{3,1},{4,6},{5,7},{6,4},{7,5},{8,10},{9,11},{10,... | collective-permute-start | bytes 10321928 | tf_op jit(solution)/shard_map/ppermute | solution.py:19
  591.2 101.9 %all-to-all-start = ((f32[16,96,560]{2,1,0:T(8,128)}), f32[16,96,560]{2,1,0:T(8,128)}, u32[]{:S(2)}, u32[]{:S(2)}) async-start(f32[16,96,560]{2,1,0:T(8,128)} %bitcast.7), calls=%async_computation | async-start | bytes 7864320 | tf_op jit(solution)/shard_map/all_to_all | solution.py:579

commit v4 on v3

--- a/solution.py
+++ b/solution.py
@@ -174,13 +174,6 @@
         def _():
             far_copy.wait_recv()
 
-        @pl.when(step == turn_at)
-        def _():
-            for copy in first[:2]:
-                copy.wait_recv()
-            for copy in second:
-                copy.start()
-
     @pl.when(fresh)
     def _():
         copies = weights(0)[1]
@@ -238,13 +231,24 @@
                 for copy in results(k, which):
                     copy.start()
 
+        if turn_at is not None and which == 0:
+            @pl.when(step == turn_at)
+            def _():
+                for copy in first[:2]:
+                    copy.wait_recv()
+                for copy in second:
+                    copy.start()
+
+            @pl.when(step == steps - 1)
+            def _():
+                for copy in second[:2]:
+                    copy.wait_recv()
+                for copy in last:
+                    copy.start()
+
     @pl.when(step == steps - 1)
     def _():
         if turn_at is not None:
-            for copy in second[:2]:
-                copy.wait_recv()
-            for copy in last:
-                copy.start()
             keep.wait()
             first[2].wait_recv()
             for copy in second[2:] + last:
@@ -560,7 +564,7 @@
         hidden1_all = [hidden1_all]
 
         far_lo, far_hi, y_lo, y_hi, z_lo, z_hi, all_grad0, grad1_all = column_grads(
-            [(hidden1_all, [grad1_all], 1, bits, True) for bits in (Y | Z, Y, Z)], w_in, w_out, grad0, 8, grad1_all, 0
+            [(hidden1_all, [grad1_all], 1, bits, True) for bits in (Y | Z, Y, Z)], w_in, w_out, grad0, 7, grad1_all, 0
         )
         grad1_all = [grad1_all]
         all_grad0 = all_grad0.reshape(all_tokens.shape)

time: 710 us -> 708 us (level)
  no operation moved by 1% of the time
where the time goes in v4:
time: 708 us; the launch traced here: 696 us
  Pallas kernels  538 us (76%)
  waiting for transfers between devices  133 us (19%)
  starting transfers between devices  15.5 us (2%)
  other arithmetic  9.49 us (1%)
    pallas_call x3, Pallas kernels, column_grads(): pl.pallas_call(functools.partial(grads_body, plan, len(arrays), len(out_s...  292 us
    pallas_call x1, Pallas kernels, run_layers(): pl.pallas_call(functools.partial(layers_body, scale, 2, tiles), grid=(3 *...  209 us
    ppermute x8, waiting for transfers between devices, swap(): return lax.ppermute(value, AXIS, [(i, i ^ bits) for i in range(DEVICES)])  90.5 us
    all_to_all x2, waiting for transfers between devices, exchange(): return lax.all_to_all(first, AXIS, split_axis=0, concat_axis=0, tiled=True)  42.1 us
    pallas_call x4, Pallas kernels, into_layer(): pl.pallas_call(functools.partial(body, len(inputs)), grid=grid, out_shape...  23.5 us
  transfers between devices with their start and end apart: 10, of which 5 were waited for; matrix products, arithmetic and copies ran while one was open for 1% of the time, Pallas kernels for 30%

profile of v4, /device:TPU:0, one launch (start us, length us, event | category | flops | bytes accessed | tf_op | source)
XLA Modules:
  0.0 696.4 jit_solution(16038899111405205228)
XLA Ops:
  0.6 209.0 %run_layers.1 = (bf16[8,1024,1536]{2,1,0:T(8,128)(2,1)}, bf16[4,1024,1536]{2,1,0:T(8,128)(2,1)}, bf16[4,1024,1536]{2,1,0:T(8,128)(2,1)}, bf16[1024,1536]{1,0:T(8,128)(2,1)}) custom-call(bf16[1024,1536]{1,0:T(8,128)(2,1)} %refs_0_.1, bf16[1024,1536]{1,0:T(8,128)(2,1)} %refs_1_.1, bf16[2,1536,8960]{2,1,0:T(8,128)(2,1)} %refs_2_.3, bf16[2,8960,1536]{2,1,0:T(8,128)(2,1)} %refs_3_.5), custom_call_target="tpu_custom_call" | custom-call | flops 169114337280 | bytes 165150720 | tf_op jit(solution)/shard_map/run_layers/pallas_call | solution.py:438
  209.7 112.6 %column_grads.3 = (f32[2,560,768]{2,1,0:T(8,128)}, f32[2,560,768]{2,1,0:T(8,128)}, f32[2,560,768]{2,1,0:T(8,128)}, f32[2,560,768]{2,1,0:T(8,128)}, f32[2,560,768...) custom-call(bf16[4096,1536]{1,0:T(8,128)(2,1)} %bitcast.12, ...), custom_call_target="tpu_custom_call", output_to_operand_aliasing={{7}: (1, {})} | custom-call | flops 84557168640 | bytes 106463232 | tf_op jit(solution)/shard_map/column_grads/pallas_call | solution.py:292
  322.3 1.1 collective-permute-start.1
  323.3 1.1 collective-permute-start.3
  324.4 72.7 %column_grads.5 = (f32[560,1536]{1,0:T(8,128)}, f32[560,1536]{1,0:T(8,128)}) custom-call(bf16[8192,1536]{1,0:T(8,128)(2,1)} %bitcast.8, bf16[8192,1536]{1,0:T(8,128)(2,1)} %bitcast.10, bf16[2,1536,8960]{2,1,0:T(8,128)(2,1)} %refs_2_.3, bf16[2,8960,1536]{2,1,0:T(8,128)(2,1)} %refs_3_.5), custom_call_target="tpu_custom_call" | custom-call | flops 56371445760 | bytes 60653568 | tf_op jit(solution)/shard_map/column_grads/pallas_call | solution.py:292
  399.6 5.3 add.6
  405.0 1.1 collective-permute-start.2
  406.1 4.2 add.7
  410.2 1.0 collective-permute-start.4
  411.3 107.1 %column_grads.4 = (f32[2,560,768]{2,1,0:T(8,128)}, f32[2,560,768]{2,1,0:T(8,128)}, f32[560,1536]{1,0:T(8,128)}, f32[560,1536]{1,0:T(8,128)}) custom-call(bf16[4096,1536]{1,0:T(8,128)(2,1)} %bitcast.13, bf16[4096,1536]{1,0:T(8,128)(2,1)} %get-tuple-element.23.refs_1_, bf16[8192,1536]{1,0:T(8,128)(2,1)} %bitcast.9, bf16[8192,1536]{1,0:T(8,128)(2,1)} %bitcast.11, ...), custom_call_target="tpu_custom_call" | custom-call | flops 84557168640 | bytes 96141312 | tf_op jit(solution)/shard_map/column_grads/pallas_call | solution.py:292
  518.3 6.1 shard_map.60
  524.4 3.3 all-to-all-start.1
  527.7 1.7 collective-permute-start.7
  529.5 35.4 %collective-permute-done.2.refs_3_ = f32[2,560,768]{2,1,0:T(8,128)} collective-permute-done((f32[2,560,768]{2,1,0:T(8,128)}, f32[2,560,768]{2,1,0:T(8,128)}, u32[]{:S(2)}, u32[]{:S(2)}) %collective-permute-start.2) | collective-permute-done | bytes 3440672 | tf_op jit(solution)/shard_map/ppermute | solution.py:19
  564.9 11.5 %collective-permute-done.4.refs_4_ = f32[2,560,768]{2,1,0:T(8,128)} collective-permute-done((f32[2,560,768]{2,1,0:T(8,128)}, f32[2,560,768]{2,1,0:T(8,128)}, u32[]{:S(2)}, u32[]{:S(2)}) %collective-permute-start.4) | collective-permute-done | bytes 3440672 | tf_op jit(solution)/shard_map/ppermute | solution.py:19
  576.4 6.9 shard_map.59
  583.3 5.6 all-to-all-done.1.blocks
  588.9 3.7 all-to-all-start
  592.7 5.2 shard_map.61.refs_0_
  597.9 6.9 shard_map.63.refs_2_
  604.8 43.6 %collective-permute-done.7.refs_1_ = f32[560,1536]{1,0:T(8,128)} collective-permute-done((f32[560,1536]{1,0:T(8,128)}, f32[560,1536]{1,0:T(8,128)}, u32[]{:S(2)}, u32[]{:S(2)}) %collective-permute-start.7) | collective-permute-done | bytes 3440672 | tf_op jit(solution)/shard_map/ppermute | solution.py:19
  648.3 6.2 shard_map.64
  654.5 36.4 %all-to-all-done.blocks = f32[16,96,560]{2,1,0:T(8,128)} async-done(((f32[16,96,560]{2,1,0:T(8,128)}), f32[16,96,560]{2,1,0:T(8,128)}, u32[]{:S(2)}, u32[]{:S(2)}) %all-to-all-start) | async-done | bytes 3440672 | tf_op jit(solution)/shard_map/all_to_all | solution.py:583
  690.9 5.2 shard_map.62
  (10 shorter events, 2.5 us)
Async XLA Ops:
  322.3 77.4 %collective-permute-start.1 = (f32[2,560,768]{2,1,0:T(8,128)}, f32[2,560,768]{2,1,0:T(8,128)}, u32[]{:S(2)}, u32[]{:S(2)}) collective-permute-start(f32[2,560,768]{2,1,0:T(8,128)} %get-tuple-element.30), channel_id=1, source_target_pairs={{0,8},{1,9},{2,10},{3,11},{4,12},{5,13},{6,14},{7,15},{8,0},{9,1},... | collective-permute-start | bytes 10321928 | tf_op jit(solution)/shard_map/ppermute | solution.py:19
  323.3 82.7 %collective-permute-start.3 = (f32[2,560,768]{2,1,0:T(8,128)}, f32[2,560,768]{2,1,0:T(8,128)}, u32[]{:S(2)}, u32[]{:S(2)}) collective-permute-start(f32[2,560,768]{2,1,0:T(8,128)} %get-tuple-element.32), channel_id=1, source_target_pairs={{0,4},{1,5},{2,6},{3,7},{4,0},{5,1},{6,2},{7,3},{8,12},{9,13},{10,... | collective-permute-start | bytes 10321928 | tf_op jit(solution)/shard_map/ppermute | solution.py:19
  397.1 121.2 %collective-permute-start.6 = (f32[560,1536]{1,0:T(8,128)}, f32[560,1536]{1,0:T(8,128)}, u32[]{:S(2)}, u32[]{:S(2)}) collective-permute-start(f32[560,1536]{1,0:T(8,128)} %get-tuple-element.35), channel_id=1, source_target_pairs={{0,2},{1,3},{2,0},{3,1},{4,6},{5,7},{6,4},{7,5},{8,10},{9,11},{10,... | collective-permute-start | bytes 10321928 | tf_op jit(solution)/shard_map/ppermute | solution.py:19
  397.7 131.8 %collective-permute-start = (f32[2,560,768]{2,1,0:T(8,128)}, f32[2,560,768]{2,1,0:T(8,128)}, u32[]{:S(2)}, u32[]{:S(2)}) collective-permute-start(f32[2,560,768]{2,1,0:T(8,128)} %get-tuple-element.28), channel_id=1, source_target_pairs={{0,4},{1,5},{2,6},{3,7},{4,0},{5,1},{6,2},{7,3},{8,12},{9,13},{10,... | collective-permute-start | bytes 10321928 | tf_op jit(solution)/shard_map/ppermute | solution.py:19
  398.7 130.8 %collective-permute-start.5 = (f32[2,560,768]{2,1,0:T(8,128)}, f32[2,560,768]{2,1,0:T(8,128)}, u32[]{:S(2)}, u32[]{:S(2)}) collective-permute-start(f32[2,560,768]{2,1,0:T(8,128)} %get-tuple-element.33), channel_id=1, source_target_pairs={{0,8},{1,9},{2,10},{3,11},{4,12},{5,13},{6,14},{7,15},{8,0},{9,1},... | collective-permute-start | bytes 10321928 | tf_op jit(solution)/shard_map/ppermute | solution.py:19
  399.6 6.4 copy-start
  405.0 159.9 %collective-permute-start.2 = (f32[2,560,768]{2,1,0:T(8,128)}, f32[2,560,768]{2,1,0:T(8,128)}, u32[]{:S(2)}, u32[]{:S(2)}) collective-permute-start(f32[2,560,768]{2,1,0:T(8,128)} %add.6), channel_id=1, source_target_pairs={{0,4},{1,5},{2,6},{3,7},{4,0},{5,1},{6,2},{7,3},{8,12},{9,13},{10,... | collective-permute-start | bytes 10321928 | tf_op jit(solution)/shard_map/ppermute | solution.py:19
  410.2 166.2 %collective-permute-start.4 = (f32[2,560,768]{2,1,0:T(8,128)}, f32[2,560,768]{2,1,0:T(8,128)}, u32[]{:S(2)}, u32[]{:S(2)}) collective-permute-start(f32[2,560,768]{2,1,0:T(8,128)} %add.7), channel_id=1, source_target_pairs={{0,8},{1,9},{2,10},{3,11},{4,12},{5,13},{6,14},{7,15},{8,0},{9,1},... | collective-permute-start | bytes 10321928 | tf_op jit(solution)/shard_map/ppermute | solution.py:19
  524.4 64.5 %all-to-all-start.1 = ((f32[16,96,560]{2,1,0:T(8,128)}), f32[16,96,560]{2,1,0:T(8,128)}, u32[]{:S(2)}, u32[]{:S(2)}) async-start(f32[16,96,560]{2,1,0:T(8,128)} %bitcast.6), calls=%async_computation.1 | async-start | bytes 7864320 | tf_op jit(solution)/shard_map/all_to_all | solution.py:583
  527.7 120.6 %collective-permute-start.7 = (f32[560,1536]{1,0:T(8,128)}, f32[560,1536]{1,0:T(8,128)}, u32[]{:S(2)}, u32[]{:S(2)}) collective-permute-start(f32[560,1536]{1,0:T(8,128)} %get-tuple-element.37), channel_id=1, source_target_pairs={{0,2},{1,3},{2,0},{3,1},{4,6},{5,7},{6,4},{7,5},{8,10},{9,11},{10,... | collective-permute-start | bytes 10321928 | tf_op jit(solution)/shard_map/ppermute | solution.py:19
  588.9 102.0 %all-to-all-start = ((f32[16,96,560]{2,1,0:T(8,128)}), f32[16,96,560]{2,1,0:T(8,128)}, u32[]{:S(2)}, u32[]{:S(2)}) async-start(f32[16,96,560]{2,1,0:T(8,128)} %bitcast.7), calls=%async_computation | async-start | bytes 7864320 | tf_op jit(solution)/shard_map/all_to_all | solution.py:583
